TPU v7x, 16 devices: a whole 2x2x2 slice. The times are simulated.
16 devices in a mesh: rep: 1, r: 2 (over z), s: 8 (over x, y, core).
Axes of the slice: x: 2, y: 2, z: 2, core: 2. Of those that a mesh axis runs over, the one named last changes fastest.
Arguments:
- x: bfloat16 [16, 4096, 896], P(('rep', 'r', 's'))
- dy: bfloat16 [16, 4096, 896], P(('rep', 'r', 's'))
- w_gate: bfloat16 [2, 896, 2560], P(None, 's')
- w_up: bfloat16 [2, 896, 2560], P(None, 's')
- w_down: bfloat16 [2, 2560, 896], P(None, 's')
- m_w_gate: float32 [2, 896, 2560], P(None, 's')
- m_w_up: float32 [2, 896, 2560], P(None, 's')
- m_w_down: float32 [2, 2560, 896], P(None, 's')
- v_w_gate: float32 [2, 896, 2560], P(None, 's')
- v_w_up: float32 [2, 896, 2560], P(None, 's')
- v_w_down: float32 [2, 2560, 896], P(None, 's')
Outputs:
- output 1: bfloat16 [2, 896, 2560], P('rep', 's')
- output 2: bfloat16 [2, 896, 2560], P('rep', 's')
- output 3: bfloat16 [2, 2560, 896], P('rep', 's')
- output 4: float32 [2, 896, 2560], P('rep', 's')
- output 5: float32 [2, 896, 2560], P('rep', 's')
- output 6: float32 [2, 2560, 896], P('rep', 's')
- output 7: float32 [2, 896, 2560], P('rep', 's')
- output 8: float32 [2, 896, 2560], P('rep', 's')
- output 9: float32 [2, 2560, 896], P('rep', 's')
All inputs are finite; a program needn't handle non-finite values.
Results may differ from a plain program's by a relative error of at most 0.022.
Values are sent between devices in bfloat16 or wider.
A program may use at most 2 GiB of HBM per device.

v0:
```python
import jax
import jax.numpy as jnp
from jax import lax
from jax.sharding import PartitionSpec as P

NAMES = ("w_gate", "w_up", "w_down")


def matmul(a, w):
    return jnp.dot(a, w, preferred_element_type=jnp.float32).astype(jnp.bfloat16)


def normed(h):
    wide = h.astype(jnp.float32)
    scale = lax.rsqrt(jnp.mean(wide**2, -1, keepdims=True) + 1e-6)
    return (wide * scale).astype(jnp.bfloat16)


def layer(h, w):
    a = normed(h)
    gate = jnp.dot(a, w["w_gate"], preferred_element_type=jnp.float32)
    up = jnp.dot(a, w["w_up"], preferred_element_type=jnp.float32)
    return h + matmul((jax.nn.silu(gate) * up).astype(jnp.bfloat16), w["w_down"])


def adamw(w, m, v, g):
    m = 0.9 * m + 0.1 * g
    v = 0.95 * v + 0.05 * g * g
    step = m * lax.rsqrt(v + 1e-8) + 0.1 * w
    return (w - 0.02 * step).astype(jnp.bfloat16), m, v


def clipped(gradients, sum_of_squares, count):
    factor = jnp.minimum(1.0, 0.5 * lax.rsqrt(sum_of_squares / count + 1e-30))
    return [g * factor for g in gradients]


def solution(mesh):
    def fetched(weights, number):
        return {name: lax.all_gather(w[number], "s", axis=0, tiled=True) for name, w in zip(NAMES, weights, strict=True)}

    def summed(term):
        return lax.psum(lax.psum_scatter(term, "s", scatter_dimension=0, tiled=True), "r")

    def step(x, dy, *arrays):
        weights, m, v = (arrays[i : i + 3] for i in (0, 3, 6))
        layers = weights[0].shape[0]
        h, kept = x[0], []
        for number in range(layers):
            kept.append(h)
            h = layer(h, fetched(weights, number))
        by_h, mine = dy[0], [None] * layers
        for number in reversed(range(layers)):
            _, back = jax.vjp(lambda w, h: layer(h, w), fetched(weights, number), kept[number])
            by_w, by_h = back(by_h)
            mine[number] = [summed(by_w[name]) for name in NAMES]
        gradients = [jnp.stack([mine[number][i] for number in range(layers)]).astype(jnp.float32) for i in range(3)]
        squares = lax.psum(sum(jnp.sum(g * g) for g in gradients), "s")
        gradients = clipped(gradients, squares, lax.psum(1, "s") * sum(g.size for g in gradients))
        new = [adamw(w.astype(jnp.float32), m, v, g) for w, m, v, g in zip(weights, m, v, gradients, strict=True)]
        return tuple(one[which] for which in range(3) for one in new)

    states, cut = P(("rep", "r", "s"), None, None), P(None, "s", None)
    return jax.shard_map(
        step,
        mesh=mesh,
        in_specs=(states, states) + (cut,) * 9,
        out_specs=(P("rep", "s", None),) * 9,
        check_vma=False,
    )
```

profile of v0, /device:TPU:0, one launch (start us, length us, event | category | flops | bytes accessed | tf_op | source)
XLA Modules:
  0.0 824.8 jit_solution(5108348797138074904)
XLA Ops:
  16.1 10.7 %copy.20 = bf16[1,4096,896]{1,2,0:T(8,128)(2,1)} copy(bf16[1,4096,896]{2,1,0:T(8,128)(2,1)} %param.11) | data formatting | bytes 14680064 | tf_op args[0]
  31.5 10.7 %copy.21 = bf16[1,4096,896]{1,2,0:T(8,128)(2,1)} copy(bf16[1,4096,896]{2,1,0:T(8,128)(2,1)} %param.12) | data formatting | bytes 14680064 | tf_op args[1]
  47.5 29.4 %fusion.44 = f32[4096,2560]{1,0:T(8,128)} fusion(bf16[1,4096,896]{1,2,0:T(8,128)(2,1)} %copy.20, f32[4096]{0:T(1024)S(1)} %add_rsqrt_fusion, bf16[1,896,2560]{2,1,0:T(8,128)(2,1)} %all-gather.13.cloned.1.call-done), kind=kOutput, calls=%fused_computation.54 | convolution fusion | flops 18801491968 | bytes 53886976 | tf_op jit(solution)/shard_map/dot_general | solution.py:21
  76.9 7.2 all-gather.15.cloned.1.call-done
  84.1 49.8 %multiply_convert_fusion.1 = (bf16[4096,2560]{1,0:T(8,128)(2,1)}, f32[4096,2560]{1,0:T(8,128)}) fusion(f32[4096,2560]{1,0:T(8,128)} %fusion.44, bf16[1,896,2560]{2,1,0:T(8,128)(2,1)} %all-gather.15.cloned.1.call-done, bf16[1,4096,896]{1,2,0:T(8,128)(2,1)} %copy.20, f32[4096]{0:T(1024)S(1)} %add_rsqrt_fusion), kind=kOutput, calls=%fused_computation.17 | convolution fusion | flops 18864406528 | bytes 116801536 | tf_op jit(solution)/shard_map/dot_general | solution.py:22
  133.9 26.8 %fusion.19 = (f32[4096]{0:T(1024)S(1)}, bf16[4096,896]{0,1:T(8,128)(2,1)}) fusion(bf16[4096,2560]{1,0:T(8,128)(2,1)} %get-tuple-element.30, bf16[1,2560,896]{2,1,0:T(8,128)(2,1)} %all-gather.17.cloned.1.call-done, bf16[1,4096,896]{1,2,0:T(8,128)(2,1)} %copy.20), kind=kOutput, calls=%fused_computation.37 | convolution fusion | flops 18808827904 | bytes 40255488 | tf_op jit(solution)/shard_map/dot_general | solution.py:10
  161.4 29.7 %fusion.36 = f32[4096,2560]{1,0:T(8,128)} fusion(bf16[4096,896]{0,1:T(8,128)(2,1)} %get-tuple-element.33, f32[4096]{0:T(1024)S(1)} %fusion.77, bf16[1,896,2560]{2,1,0:T(8,128)(2,1)} %all-gather.23.cloned.1.call-done), kind=kOutput, calls=%fused_computation.51 | convolution fusion | flops 18801491968 | bytes 53886976 | tf_op jit(solution)/shard_map/jvp()/dot_general | solution.py:22
  193.8 28.4 %convolution_convert_fusion.1 = bf16[4096,2560]{1,0:T(8,128)(2,1)} fusion(bf16[1,4096,896]{2,1,0:T(8,128)(2,1)} %param.12, bf16[1,2560,896]{2,1,0:T(8,128)(2,1)} %all-gather.21.cloned.1.call-done), kind=kOutput, calls=%fused_computation.27 | convolution fusion | flops 18800967680 | bytes 32899072 | tf_op jit(solution)/shard_map/transpose(jvp())/dot_general | solution.py:10
  222.2 8.1 all-gather.19.cloned.1.call-done
  230.3 58.3 %fusion.2 = (bf16[4096,2560]{1,0:T(8,128)(2,1)}, f32[4096,2560]{1,0:T(8,128)}) fusion(f32[4096,2560]{1,0:T(8,128)} %fusion.36, bf16[4096,2560]{1,0:T(8,128)(2,1)} %convolution_convert_fusion.1, bf16[1,896,2560]{2,1,0:T(8,128)(2,1)} %all-gather.19.cloned.1.call-done, bf16[4096,896]{0,1:T(8,128)(2,1)} %get-tuple-element.33, f32[4096]{0:T(1024)S(1)} %fusion.77), kind=kOutput, calls=%fused_computation.8 | convolution fusion | flops 18927321088 | bytes 137773056 | tf_op jit(solution)/shard_map/jvp()/dot_general | solution.py:21
  288.6 23.5 %fusion.49 = bf16[4096,896]{0,1:T(8,128)(2,1)} fusion(bf16[4096,2560]{1,0:T(8,128)(2,1)} %get-tuple-element.34, bf16[1,896,2560]{2,1,0:T(8,128)(2,1)S(1)} %copy-done.18), kind=kOutput, calls=%fused_computation.58 | convolution fusion | flops 18790481920 | bytes 32899072 | tf_op jit(solution)/shard_map/transpose(jvp())/dot_general | solution.py:21
  312.1 38.3 %fusion.21 = (f32[4096]{0:T(1024)S(1)}, bf16[4096,896]{0,1:T(8,128)(2,1)}) fusion(bf16[4096,896]{0,1:T(8,128)(2,1)} %get-tuple-element.33, bf16[4096,896]{0,1:T(8,128)(2,1)} %fusion.49, bf16[1,896,2560]{2,1,0:T(8,128)(2,1)} %all-gather.23.cloned.1.call-done, bf16[4096,2560]{1,0:T(8,128)(2,1)} %convolution_convert_fusion.1, f32[4096,2560]{1,0:T(8,128)} %get-tuple-element.35), kind=kOutput, calls=%fused_computation.39 | convolution fusion | flops 18875412480 | bytes 89538560 | tf_op jit(solution)/shard_map/transpose(jvp())/dot_general | solution.py:22
  350.4 9.8 %fusion.22 = bf16[4096,896]{0,1:T(8,128)(2,1)S(1)} fusion(bf16[4096,896]{0,1:T(8,128)(2,1)} %get-tuple-element.33, bf16[4096,896]{0,1:T(8,128)(2,1)} %get-tuple-element.37, bf16[1,4096,896]{1,2,0:T(8,128)(2,1)} %copy.21, f32[4096]{0:T(1024)S(1)} %multiply_multiply_fusion.3, f32[4096]{0:T(1024)S(1)} %fusion.77), kind=kLoop, calls=%fused_computation.40 | loop fusion | flops 25690112 | bytes 29392896 | tf_op jit(solution)/shard_map/transpose(jvp())/add_any | solution.py:14
  363.2 26.4 %convolution_convert_fusion.2 = bf16[2560,896]{1,0:T(8,128)(2,1)} fusion(bf16[4096,2560]{1,0:T(8,128)(2,1)} %get-tuple-element.30, bf16[4096,896]{0,1:T(8,128)(2,1)S(1)} %fusion.22), kind=kOutput, calls=%fused_computation.49 | convolution fusion | flops 18792775680 | bytes 32899072 | tf_op jit(solution)/shard_map/transpose(jvp())/dot_general | solution.py:10
  389.7 36.1 %fusion.26 = bf16[2560,896]{1,0:T(8,128)(2,1)} fusion(bf16[1,4096,896]{2,1,0:T(8,128)(2,1)} %param.12, f32[4096,2560]{1,0:T(8,128)} %fusion.36, f32[4096,2560]{1,0:T(8,128)} %get-tuple-element.35), kind=kOutput, calls=%fused_computation.45 | convolution fusion | flops 18855690240 | bytes 95813632 | tf_op jit(solution)/shard_map/transpose(jvp())/dot_general | solution.py:10
  425.9 27.7 %convolution_convert_fusion = bf16[4096,2560]{1,0:T(8,128)(2,1)} fusion(bf16[4096,896]{0,1:T(8,128)(2,1)} %copy-done, bf16[1,2560,896]{2,1,0:T(8,128)(2,1)} %all-gather.17.cloned.1.call-done), kind=kOutput, calls=%fused_computation.26 | convolution fusion | flops 18800967680 | bytes 32899072 | tf_op jit(solution)/shard_map/transpose(jvp())/dot_general | solution.py:10
  453.6 34.0 %fusion.33 = bf16[896,2560]{1,0:T(8,128)(2,1)} fusion(bf16[4096,2560]{1,0:T(8,128)(2,1)} %convolution_convert_fusion, f32[4096,2560]{1,0:T(8,128)} %fusion.44, bf16[1,4096,896]{1,2,0:T(8,128)(2,1)} %copy.20, f32[4096]{0:T(1024)S(1)} %copy-done.17), kind=kOutput, calls=%fused_computation.48 | convolution fusion | flops 18866700288 | bytes 74858496 | tf_op jit(solution)/shard_map/transpose(jvp())/dot_general | solution.py:22
  487.7 34.6 %fusion.29 = bf16[896,2560]{1,0:T(8,128)(2,1)} fusion(bf16[4096,2560]{1,0:T(8,128)(2,1)} %convolution_convert_fusion.1, bf16[4096,896]{0,1:T(8,128)(2,1)} %get-tuple-element.33, f32[4096]{0:T(1024)S(1)} %copy-done.13, f32[4096,2560]{1,0:T(8,128)} %get-tuple-element.35), kind=kOutput, calls=%fused_computation.46 | convolution fusion | flops 18866700288 | bytes 74858496 | tf_op jit(solution)/shard_map/transpose(jvp())/dot_general | solution.py:22
  522.3 42.3 %fusion.30 = bf16[896,2560]{1,0:T(8,128)(2,1)} fusion(f32[4096,2560]{1,0:T(8,128)} %fusion.44, f32[4096,2560]{1,0:T(8,128)} %get-tuple-element.31, bf16[4096,2560]{1,0:T(8,128)(2,1)} %convolution_convert_fusion, bf16[1,4096,896]{1,2,0:T(8,128)(2,1)} %copy.20, f32[4096]{0:T(1024)S(1)} %copy-done.17), kind=kOutput, calls=%fused_computation.47 | convolution fusion | flops 18919129088 | bytes 116801536 | tf_op jit(solution)/shard_map/transpose(jvp())/dot_general | solution.py:21
  564.7 25.3 %convolution_convert_fusion.3 = bf16[896,2560]{1,0:T(8,128)(2,1)} fusion(bf16[4096,2560]{1,0:T(8,128)(2,1)} %get-tuple-element.34, bf16[4096,896]{0,1:T(8,128)(2,1)} %get-tuple-element.33, f32[4096]{0:T(1024)S(1)} %copy-done.13), kind=kOutput, calls=%fused_computation.50 | convolution fusion | flops 18801491968 | bytes 32915456 | tf_op jit(solution)/shard_map/transpose(jvp())/dot_general | solution.py:21
  590.2 49.0 %reduce-scatter.7.cloned.1.call-done = bf16[112,2560]{1,0:T(8,128)(2,1)} async-done(((bf16[896,2560]{1,0:T(8,128)(2,1)}), bf16[112,2560]{1,0:T(8,128)(2,1)}) %reduce-scatter.7.cloned.1.call-update) | async-done | bytes 573456 | tf_op jit(solution)/shard_map/reduce_scatter | solution.py:43
  639.2 50.5 %reduce-scatter.9.cloned.1.call-done = bf16[112,2560]{1,0:T(8,128)(2,1)} async-done(((bf16[896,2560]{1,0:T(8,128)(2,1)}), bf16[112,2560]{1,0:T(8,128)(2,1)}) %reduce-scatter.9.cloned.1.call-update) | async-done | bytes 573456 | tf_op jit(solution)/shard_map/reduce_scatter | solution.py:43
  689.6 91.0 %all-reduce.3.cloned.1.call-done = (bf16[1,112,2560]{2,1,0:T(8,128)(2,1)}, bf16[1,112,2560]{2,1,0:T(8,128)(2,1)}, bf16[1,112,2560]{2,1,0:T(8,128)(2,1)}, bf16[1,...) async-done(((bf16[1,112,2560]{2,1,0:T(8,128)(2,1)}, bf16[1,112,2560]{2,1,0:T(8,128)(2,1)}, bf16[1,112,2560]{2,1,0:T(8,128)(2,1)}, ...) | async-done | bytes 3440656 | tf_op jit(solution)/shard_map/psum | solution.py:43
  790.0 13.8 %psum.55 = f32[]{:T(128)} all-reduce(f32[]{:T(128)S(6)} %add.111), channel_id=1, replica_groups=mesh['rep'=1,'r'=2,'s'=8] {'s'}, use_global_device_ids=true, to_apply=%region_18.19 | all-reduce | flops 1 | bytes 8 | tf_op jit(solution)/shard_map/psum | solution.py:58
  (84 shorter events, 46.4 us)
Async XLA Ops:
  7.2 40.3 %all-gather.13.cloned.1.call-start = ((), (), s32[]{:S(2)}) async-start(), calls=%async_computation.12 | async-start | bytes 5160960 | tf_op jit(solution)/shard_map/all_gather | solution.py:40
  9.6 74.6 %all-gather.15.cloned.1.call-start = ((), (), s32[]{:S(2)}) async-start(), calls=%async_computation.13 | async-start | bytes 5160960 | tf_op jit(solution)/shard_map/all_gather | solution.py:40
  11.9 122.0 %all-gather.17.cloned.1.call-start = ((), (), s32[]{:S(2)}) async-start(), calls=%async_computation.14 | async-start | bytes 5160960 | tf_op jit(solution)/shard_map/all_gather | solution.py:40
  14.3 147.0 %all-gather.23.cloned.1.call-start = ((), (), s32[]{:S(2)}) async-start(), calls=%async_computation.17 | async-start | bytes 5160960 | tf_op jit(solution)/shard_map/all_gather | solution.py:40
  14.9 178.9 %all-gather.21.cloned.1.call-start = ((), (), s32[]{:S(2)}) async-start(), calls=%async_computation.16 | async-start | bytes 5160960 | tf_op jit(solution)/shard_map/all_gather | solution.py:40
  15.5 214.8 %all-gather.19.cloned.1.call-start = ((), (), s32[]{:S(2)}) async-start(), calls=%async_computation.15 | async-start | bytes 5160960 | tf_op jit(solution)/shard_map/all_gather | solution.py:40
  16.1 574.0 %reduce-scatter.15.cloned.1.call-start = ((), (), s32[]{:S(2)}) async-start(), calls=%async_computation.10 | async-start | bytes 5160960 | tf_op jit(solution)/shard_map/reduce_scatter | solution.py:43
  31.4 52.7 %copy-start.16 = (f32[4096]{0:T(1024)}, f32[4096]{0:T(1024)S(1)}, u32[]{:S(2)}) copy-start(f32[4096]{0:T(1024)S(1)} %add_rsqrt_fusion) | copy-start | bytes 49156
  161.3 189.0 %copy-start.12 = (f32[4096]{0:T(1024)}, f32[4096]{0:T(1024)S(1)}, u32[]{:S(2)}) copy-start(f32[4096]{0:T(1024)S(1)} %fusion.77) | copy-start | bytes 49156
  230.3 58.3 %copy-start.18 = (bf16[1,896,2560]{2,1,0:T(8,128)(2,1)S(1)}, bf16[1,896,2560]{2,1,0:T(8,128)(2,1)}, u32[]{:S(2)}) copy-start(bf16[1,896,2560]{2,1,0:T(8,128)(2,1)} %all-gather.19.cloned.1.call-done) | copy-start | bytes 13762564
  312.1 38.3 %copy-start.15 = (f32[4096]{0:T(1024)S(1)}, f32[4096]{0:T(1024)}, u32[]{:S(2)}) copy-start(f32[4096]{0:T(1024)} %copy-done.14) | copy-start | bytes 49156
  389.6 200.5 %reduce-scatter.17.cloned.1.call-start = ((), (), s32[]{:S(2)}) async-start(), calls=%async_computation.11 | async-start | bytes 5160960 | tf_op jit(solution)/shard_map/reduce_scatter | solution.py:43
  425.8 27.8 %copy-start.17 = (f32[4096]{0:T(1024)S(1)}, f32[4096]{0:T(1024)}, u32[]{:S(2)}) copy-start(f32[4096]{0:T(1024)} %copy-done.16) | copy-start | bytes 49156
  425.8 164.4 %reduce-scatter.11.cloned.1.call-start = ((), (), s32[]{:S(2)}) async-start(), calls=%async_computation.8 | async-start | bytes 5160960 | tf_op jit(solution)/shard_map/reduce_scatter | solution.py:43
  453.6 34.1 %copy-start.13 = (f32[4096]{0:T(1024)S(1)}, f32[4096]{0:T(1024)}, u32[]{:S(2)}) copy-start(f32[4096]{0:T(1024)} %copy-done.12) | copy-start | bytes 49156
  487.6 102.6 %reduce-scatter.13.cloned.1.call-start = ((), (), s32[]{:S(2)}) async-start(), calls=%async_computation.9 | async-start | bytes 5160960 | tf_op jit(solution)/shard_map/reduce_scatter | solution.py:43
  522.3 116.9 %reduce-scatter.7.cloned.1.call-start = ((), (), s32[]{:S(2)}) async-start(), calls=%async_computation.6 | async-start | bytes 5160960 | tf_op jit(solution)/shard_map/reduce_scatter | solution.py:43
  564.6 125.0 %reduce-scatter.9.cloned.1.call-start = ((), (), s32[]{:S(2)}) async-start(), calls=%async_computation.7 | async-start | bytes 5160960 | tf_op jit(solution)/shard_map/reduce_scatter | solution.py:43
  590.0 214.5 %copy-start.1 = (bf16[2,320,896]{2,1,0:T(8,128)(2,1)S(1)}, bf16[2,320,896]{2,1,0:T(8,128)(2,1)}, u32[]{:S(2)}) copy-start(bf16[2,320,896]{2,1,0:T(8,128)(2,1)} %param.15) | copy-start | bytes 3440644
  590.0 190.6 %all-reduce.3.cloned.1.call-start = ((), (), s32[]{:S(2)}) async-start(), calls=%async_computation.18 | async-start | bytes 6881280 | tf_op jit(solution)/shard_map/psum | solution.py:43
  783.1 27.8 %copy-start.2 = (bf16[2,112,2560]{2,1,0:T(8,128)(2,1)S(1)}, bf16[2,112,2560]{2,1,0:T(8,128)(2,1)}, u32[]{:S(2)}) copy-start(bf16[2,112,2560]{2,1,0:T(8,128)(2,1)} %param.13) | copy-start | bytes 3440644
  783.1 27.8 %copy-start.3 = (bf16[2,112,2560]{2,1,0:T(8,128)(2,1)S(1)}, bf16[2,112,2560]{2,1,0:T(8,128)(2,1)}, u32[]{:S(2)}) copy-start(bf16[2,112,2560]{2,1,0:T(8,128)(2,1)} %param.14) | copy-start | bytes 3440644
  804.6 7.7 copy-start.10
  804.6 7.9 copy-start.11
  (8 other events, 44.9 us)
Sparse Core Ops, SparseCore 0:
  10.4 37.0 all-gather.12
  49.9 34.1 all-gather.14
  86.5 34.1 all-gather.16
  123.0 34.1 all-gather.22
  159.5 34.1 all-gather.20
  196.1 34.1 all-gather.18
  389.7 47.1 reduce-scatter.14
  440.3 47.1 reduce-scatter.16
  491.0 47.1 reduce-scatter.10
  541.4 47.1 reduce-scatter.12
  592.0 47.1 reduce-scatter.6
  642.5 47.1 reduce-scatter.8
  692.3 88.2 all-reduce.2
where the time goes:
time: 832 us; the launch traced here: 825 us
  matrix products  511 us (61%)
  waiting for transfers between devices  216 us (26%)
  local copies, waits for them, and re-layouts  33.7 us (4%)
  other arithmetic  33.6 us (4%)
  between operations  17 us (2%)
  blocking collectives  13.8 us (2%)
    dot_general x5, matrix products, layer(): up = jnp.dot(a, w['w_up'], preferred_element_type=jnp.float32)  186 us
    dot_general x5, matrix products, layer(): gate = jnp.dot(a, w['w_gate'], preferred_element_type=jnp.float32)  179 us
    dot_general x5, matrix products, matmul(): jnp.dot(a, w, preferred_element_type=jnp.float32).astype(jnp.bfloat16)  145 us
    reduce_scatter x6, waiting for transfers between devices, summed(): lax.psum_scatter(term, 's', scatter_dimension=0, tiled=True)  99.5 us
    psum x1, waiting for transfers between devices, summed(): lax.psum(lax.psum_scatter(term, 's', scatter_dimension=0, tiled=True), 'r')  91 us
    unnamed x40, local copies, waits for them, and re-layouts  26.8 us
    all_gather x6, waiting for transfers between devices, fetched(): lax.all_gather(w[number], 's', axis=0, tiled=True)  23.4 us
  transfers between devices with their start and end apart: 13, of which 7 were waited for; matrix products, arithmetic and copies ran while one was open for 48% of the time, Pallas kernels for 0%

commit v1 on v0

v1 whole, which is shorter than its diff:
```python
import functools

import jax
import jax.numpy as jnp
from jax import lax
from jax.experimental import pallas as pl
from jax.experimental.pallas import tpu as pltpu
from jax.sharding import PartitionSpec as P

NAMES = ("w_gate", "w_up", "w_down")
bf16, f32 = jnp.bfloat16, jnp.float32
CH, SUB, TM, LANES = 256, 512, 1024, 128
NT_DIMS = (((1,), (1,)), ((), ()))
TN_DIMS = (((0,), (0,)), ((), ()))
VMEM_LIMIT = 67043328


def groups_of(i):
    j, half = i // 2, i % 2
    first = j + 10 * half
    return first * LANES, (first + 5) * LANES


def dot(a, b):
    return jnp.dot(a, b, preferred_element_type=f32)


def rows_at(start, size, multiple=None):
    return pl.ds(pl.multiple_of(start, multiple or size), size)


def sigmoid(x):
    return 1.0 / (1.0 + jnp.exp(-x))


def columns_in(w_hbm, buf, sem, i, offset):
    return [
        pltpu.make_async_copy(w_hbm.at[:, rows_at(start, LANES)], buf.at[:, pl.ds(offset + LANES * n, LANES)], sem.at[n])
        for n, start in enumerate(groups_of(i))
    ]


def rows_in(w_hbm, buf, sem, i):
    return [
        pltpu.make_async_copy(w_hbm.at[rows_at(start, LANES), :], buf.at[pl.ds(LANES * n, LANES), :], sem.at[n])
        for n, start in enumerate(groups_of(i))
    ]


def start(copies):
    for c in copies:
        c.start()


def wait(copies):
    for c in copies:
        c.wait()


def normed_in_place(a_ref, aT_ref, t):
    rows = rows_at(t * 256, 256)
    w = a_ref[rows, :].astype(f32)
    a = (w * lax.rsqrt(jnp.mean(w * w, -1, keepdims=True) + 1e-6)).astype(bf16)
    a_ref[rows, :] = a
    if aT_ref is not None:
        aT_ref[:, rows] = a.T


def forward_kernel(h_hbm, wg_hbm, wu_hbm, wd_hbm, gu_hbm, out_hbm, a_ref, act_ref, wgu, wd, gus, hin, hout, hsem, wsem, wdsem, gsem, xsem, osem):
    T, D = a_ref.shape
    F = act_ref.shape[1]
    NC, NT = F // CH, T // TM

    def loads(t):
        rows = rows_at(t * 256, 256)
        return [pltpu.make_async_copy(h_hbm.at[rows, :], a_ref.at[rows, :], hsem.at[t])]

    def weights(i):
        slot = i % 2
        return columns_in(wg_hbm, wgu.at[slot], wsem.at[slot, 0], i, 0) + columns_in(wu_hbm, wgu.at[slot], wsem.at[slot, 1], i, CH)

    def saves(n):
        i, t = n // NT, n % NT
        return [pltpu.make_async_copy(gus.at[n % 2], gu_hbm.at[i, rows_at(t * TM, TM), :], gsem.at[n % 2])]

    def downs(i):
        return rows_in(wd_hbm, wd.at[rows_at(i * CH, CH), :], wdsem.at[i], i)

    lax.fori_loop(0, T // 256, lambda t, _: start(loads(t)) or 0, 0)
    start(weights(0))

    def norm(t, _):
        wait(loads(t))
        normed_in_place(a_ref, None, t)
        return 0

    lax.fori_loop(0, T // 256, norm, 0)
    lax.fori_loop(0, NC, lambda i, _: start(downs(i)) or 0, 0)

    def chunk(i, _):
        slot = i % 2
        wait(weights(i))

        @pl.when(i + 1 < NC)
        def _():
            start(weights(i + 1))

        def tile(t, _):
            n = i * NT + t

            @pl.when(n >= 2)
            def _():
                wait(saves(n - 2))

            def dots(k):
                gu = dot(a_ref[rows_at(t * TM + k * SUB, SUB), :], wgu[slot])
                gus[n % 2, pl.ds(k * SUB, SUB), :] = gu
                return gu

            def elementwise(k, gu):
                gate, up = gu[:, :CH], gu[:, CH:]
                act_ref[rows_at(t * TM + k * SUB, SUB), rows_at(i * CH, CH)] = (gate * sigmoid(gate) * up).astype(bf16)

            gu = dots(0)
            for k in range(TM // SUB):
                following = dots(k + 1) if k + 1 < TM // SUB else None
                elementwise(k, gu)
                gu = following
            start(saves(n))
            return 0

        lax.fori_loop(0, NT, tile, 0)
        return 0

    lax.fori_loop(0, NC, chunk, 0)
    lax.fori_loop(0, NC, lambda i, _: wait(downs(i)) or 0, 0)

    def inputs(t):
        return [pltpu.make_async_copy(h_hbm.at[rows_at(t * SUB, SUB), :], hin.at[t % 2], xsem.at[t % 2])]

    def outputs(t):
        return [pltpu.make_async_copy(hout.at[t % 2], out_hbm.at[rows_at(t * SUB, SUB), :], osem.at[t % 2])]

    start(inputs(0))

    def down(t, _):
        wait(inputs(t))

        @pl.when(t + 1 < T // SUB)
        def _():
            start(inputs(t + 1))

        @pl.when(t >= 2)
        def _():
            wait(outputs(t - 2))

        out = dot(act_ref[rows_at(t * SUB, SUB), :], wd[...]).astype(bf16)
        hout[t % 2] = (hin[t % 2].astype(f32) + out.astype(f32)).astype(bf16)
        start(outputs(t))
        return 0

    lax.fori_loop(0, T // SUB, down, 0)
    for n in (NC * NT - 2, NC * NT - 1):
        wait(saves(n))
    for t in (T // SUB - 2, T // SUB - 1):
        wait(outputs(t))


def middle_kernel(h_hbm, dy_hbm, wg_hbm, wu_hbm, wd_hbm, dwg_hbm, dwu_hbm, dwd_hbm, dh_hbm,
                  a_ref, aT_ref, dy_ref, da_ref, dgu_ref, act_ref, wgu, wd, ob, obd, hsem, ysem, wsem, osem):
    T, D = a_ref.shape
    F = dwg_hbm.shape[1]
    NC, NT = F // CH, T // TM

    def loads(t):
        rows = rows_at(t * 256, 256)
        return [pltpu.make_async_copy(h_hbm.at[rows, :], a_ref.at[rows, :], hsem.at[t])]

    def dys():
        return [pltpu.make_async_copy(dy_hbm, dy_ref, ysem)]

    def weights(i):
        slot = i % 2
        return (
            columns_in(wg_hbm, wgu.at[slot], wsem.at[slot, 0], i, 0)
            + columns_in(wu_hbm, wgu.at[slot], wsem.at[slot, 1], i, CH)
            + rows_in(wd_hbm, wd.at[slot], wsem.at[slot, 2], i)
        )

    def outs(i):
        slot = i % 2
        copies = []
        for n, at in enumerate(groups_of(i)):
            cols = rows_at(at, LANES)
            copies += [
                pltpu.make_async_copy(ob.at[slot, :, pl.ds(LANES * n, LANES)], dwg_hbm.at[:, cols], osem.at[slot, 0, n]),
                pltpu.make_async_copy(ob.at[slot, :, pl.ds(CH + LANES * n, LANES)], dwu_hbm.at[:, cols], osem.at[slot, 1, n]),
                pltpu.make_async_copy(obd.at[slot, pl.ds(LANES * n, LANES), :], dwd_hbm.at[cols, :], osem.at[slot, 2, n]),
            ]
        return copies

    lax.fori_loop(0, T // 256, lambda t, _: start(loads(t)) or 0, 0)
    start(weights(0))
    start(dys())

    def norm(t, _):
        wait(loads(t))
        normed_in_place(a_ref, aT_ref, t)
        da_ref[rows_at(t * 256, 256), :] = jnp.zeros((256, D), f32)
        return 0

    lax.fori_loop(0, T // 256, norm, 0)
    wait(dys())

    def chunk(i, _):
        slot = i % 2
        wait(weights(i))

        @pl.when(i + 1 < NC)
        def _():
            start(weights(i + 1))

        def tile(t, _):
            def rows_of(k):
                return rows_at(t * TM + k * SUB, SUB)

            def dots(k):
                rows = rows_of(k)
                return dot(a_ref[rows, :], wgu[slot]), lax.dot_general(dy_ref[rows, :], wd[slot], NT_DIMS, preferred_element_type=f32)

            def elementwise(k, gu, dact):
                rows = rows_of(k)
                dact = dact.astype(bf16).astype(f32)
                gate, up = gu[:, :CH], gu[:, CH:]
                sg = sigmoid(gate)
                silu = gate * sg
                act_ref[rows, :] = (silu * up).astype(bf16)
                dgate = (dact * up * (sg * (1.0 + gate * (1.0 - sg)))).astype(bf16)
                dup = (dact * silu).astype(bf16)
                dgu_ref[rows, pl.ds(0, CH)] = dgate
                dgu_ref[rows, pl.ds(CH, CH)] = dup
                return jnp.concatenate([dgate, dup], 1)

            def back(k, dgu):
                da_ref[rows_of(k), :] += lax.dot_general(dgu, wgu[slot], NT_DIMS, preferred_element_type=f32)

            now, before = dots(0), None
            for k in range(TM // SUB):
                following = dots(k + 1) if k + 1 < TM // SUB else None
                dgu = elementwise(k, *now)
                if before is not None:
                    back(k - 1, before)
                before, now = dgu, following
            back(TM // SUB - 1, before)
            return 0

        lax.fori_loop(0, NT, tile, 0)

        @pl.when(i >= 2)
        def _():
            wait(outs(i - 2))

        ob[slot] = dot(aT_ref[...], dgu_ref[...]).astype(bf16)
        obd[slot] = lax.dot_general(act_ref[...], dy_ref[...], TN_DIMS, preferred_element_type=f32).astype(bf16)
        start(outs(i))
        return 0

    lax.fori_loop(0, NC, chunk, 0)
    lax.fori_loop(0, T // 256, lambda t, _: start(loads(t)) or 0, 0)

    def stores(t):
        rows = rows_at(t * 256, 256)
        return [pltpu.make_async_copy(dy_ref.at[rows, :], dh_hbm.at[rows, :], hsem.at[t])]

    def norm_back(t, _):
        rows = rows_at(t * 256, 256)
        wait(loads(t))
        w = a_ref[rows, :].astype(f32)
        da = da_ref[rows, :].astype(bf16).astype(f32)
        scale = lax.rsqrt(jnp.mean(w * w, -1, keepdims=True) + 1e-6)
        along = jnp.sum(da * w, -1, keepdims=True) * (scale * scale * scale) * (1.0 / D)
        by_h = (da * scale - w * along).astype(bf16)
        dy_ref[rows, :] = (dy_ref[rows, :].astype(f32) + by_h.astype(f32)).astype(bf16)
        start(stores(t))
        return 0

    lax.fori_loop(0, T // 256, norm_back, 0)
    lax.fori_loop(0, T // 256, lambda t, _: wait(stores(t)) or 0, 0)
    for i in (NC - 2, NC - 1):
        wait(outs(i))


def last_kernel(h_hbm, dy_hbm, gu_hbm, wd_hbm, dwg_hbm, dwu_hbm, dwd_hbm,
                a_ref, aT_ref, dy_ref, dgu_ref, act_ref, gus, wd, ob, obd, hsem, ysem, gsem, wsem, osem):
    T, D = a_ref.shape
    F = dwg_hbm.shape[1]
    NC, NT = F // CH, T // TM

    def loads(t):
        rows = rows_at(t * 256, 256)
        return [pltpu.make_async_copy(h_hbm.at[rows, :], a_ref.at[rows, :], hsem.at[t])]

    def dys():
        return [pltpu.make_async_copy(dy_hbm, dy_ref, ysem)]

    def weights(i):
        slot = i % 2
        return rows_in(wd_hbm, wd.at[slot], wsem.at[slot], i)

    def kept(n):
        i, t = n // NT, n % NT
        return [pltpu.make_async_copy(gu_hbm.at[i, rows_at(t * TM, TM), :], gus.at[n % 2], gsem.at[n % 2])]

    def outs(i):
        slot = i % 2
        copies = []
        for n, at in enumerate(groups_of(i)):
            cols = rows_at(at, LANES)
            copies += [
                pltpu.make_async_copy(ob.at[slot, :, pl.ds(LANES * n, LANES)], dwg_hbm.at[:, cols], osem.at[slot, 0, n]),
                pltpu.make_async_copy(ob.at[slot, :, pl.ds(CH + LANES * n, LANES)], dwu_hbm.at[:, cols], osem.at[slot, 1, n]),
                pltpu.make_async_copy(obd.at[slot, pl.ds(LANES * n, LANES), :], dwd_hbm.at[cols, :], osem.at[slot, 2, n]),
            ]
        return copies

    lax.fori_loop(0, T // 256, lambda t, _: start(loads(t)) or 0, 0)
    start(weights(0))
    start(dys())
    start(kept(0))

    def norm(t, _):
        wait(loads(t))
        normed_in_place(a_ref, aT_ref, t)
        return 0

    lax.fori_loop(0, T // 256, norm, 0)
    wait(dys())

    def chunk(i, _):
        slot = i % 2
        wait(weights(i))

        @pl.when(i + 1 < NC)
        def _():
            start(weights(i + 1))

        def tile(t, _):
            n = i * NT + t
            wait(kept(n))

            @pl.when(n + 1 < NC * NT)
            def _():
                start(kept(n + 1))

            def rows_of(k):
                return rows_at(t * TM + k * SUB, SUB)

            def dots(k):
                return lax.dot_general(dy_ref[rows_of(k), :], wd[slot], NT_DIMS, preferred_element_type=f32)

            def elementwise(k, dact):
                rows = rows_of(k)
                dact = dact.astype(bf16).astype(f32)
                gate, up = gus[n % 2, pl.ds(k * SUB, SUB), pl.ds(0, CH)], gus[n % 2, pl.ds(k * SUB, SUB), pl.ds(CH, CH)]
                sg = sigmoid(gate)
                silu = gate * sg
                act_ref[rows, :] = (silu * up).astype(bf16)
                dgu_ref[rows, pl.ds(0, CH)] = (dact * up * (sg * (1.0 + gate * (1.0 - sg)))).astype(bf16)
                dgu_ref[rows, pl.ds(CH, CH)] = (dact * silu).astype(bf16)

            now = dots(0)
            for k in range(TM // SUB):
                following = dots(k + 1) if k + 1 < TM // SUB else None
                elementwise(k, now)
                now = following
            return 0

        lax.fori_loop(0, NT, tile, 0)

        @pl.when(i >= 2)
        def _():
            wait(outs(i - 2))

        ob[slot] = dot(aT_ref[...], dgu_ref[...]).astype(bf16)
        obd[slot] = lax.dot_general(act_ref[...], dy_ref[...], TN_DIMS, preferred_element_type=f32).astype(bf16)
        start(outs(i))
        return 0

    lax.fori_loop(0, NC, chunk, 0)
    for i in (NC - 2, NC - 1):
        wait(outs(i))


def call(kernel, outs, scratch, inputs, **params):
    anywhere = pl.BlockSpec(memory_space=pl.ANY)
    return pl.pallas_call(
        kernel,
        out_shape=[jax.ShapeDtypeStruct(*o) for o in outs],
        in_specs=[anywhere] * len(inputs),
        out_specs=[anywhere] * len(outs),
        scratch_shapes=scratch,
        compiler_params=pltpu.CompilerParams(vmem_limit_bytes=VMEM_LIMIT, **params),
    )(*inputs)


def forward(h, wg, wu, wd):
    (T, D), F = h.shape, wg.shape[1]
    V, S = pltpu.VMEM, pltpu.SemaphoreType.DMA
    return call(
        forward_kernel,
        [((F // CH, T, 2 * CH), f32), ((T, D), bf16)],
        [V((T, D), bf16), V((T, F), bf16), V((2, D, 2 * CH), bf16), V((F, D), bf16), V((2, TM, 2 * CH), f32), V((2, SUB, D), bf16), V((2, SUB, D), bf16)]
        + [S((T // 256,)), S((2, 2, 2)), S((F // CH, 2)), S((2,)), S((2,)), S((2,))],
        (h, wg, wu, wd),
    )


def middle(h, dy, wg, wu, wd):
    (T, D), F = h.shape, wg.shape[1]
    V, S = pltpu.VMEM, pltpu.SemaphoreType.DMA
    return call(
        middle_kernel,
        [((D, F), bf16), ((D, F), bf16), ((F, D), bf16), ((T, D), bf16)],
        [V((T, D), bf16), V((D, T), bf16), V((T, D), bf16), V((T, D), f32), V((T, 2 * CH), bf16), V((T, CH), bf16)]
        + [V((2, D, 2 * CH), bf16), V((2, CH, D), bf16), V((2, D, 2 * CH), bf16), V((2, CH, D), bf16)]
        + [S((T // 256,)), S(()), S((2, 3, 2)), S((2, 3, 2))],
        (h, dy, wg, wu, wd),
    )


def last(h, dy, gu, wd):
    (T, D), F = h.shape, wd.shape[0]
    V, S = pltpu.VMEM, pltpu.SemaphoreType.DMA
    return call(
        last_kernel,
        [((D, F), bf16), ((D, F), bf16), ((F, D), bf16)],
        [V((T, D), bf16), V((D, T), bf16), V((T, D), bf16), V((T, 2 * CH), bf16), V((T, CH), bf16), V((2, TM, 2 * CH), f32)]
        + [V((2, CH, D), bf16), V((2, D, 2 * CH), bf16), V((2, CH, D), bf16)]
        + [S((T // 256,)), S(()), S((2,)), S((2, 2)), S((2, 3, 2))],
        (h, dy, gu, wd),
    )


def adamw(w, m, v, g):
    m = 0.9 * m + 0.1 * g
    v = 0.95 * v + 0.05 * g * g
    step = m * lax.rsqrt(v + 1e-8) + 0.1 * w
    return (w - 0.02 * step).astype(bf16), m, v


def clipped(gradients, sum_of_squares, count):
    factor = jnp.minimum(1.0, 0.5 * lax.rsqrt(sum_of_squares / count + 1e-30))
    return [g * factor for g in gradients]


def solution(mesh):
    def fetched(weights, number):
        return [lax.all_gather(w[number], "s", axis=0, tiled=True) for w in weights]

    def summed(term):
        return lax.psum(lax.psum_scatter(term, "s", scatter_dimension=0, tiled=True), "r")

    def step(x, dy, *arrays):
        weights, m, v = (arrays[i : i + 3] for i in (0, 3, 6))
        first, second = fetched(weights, 0), fetched(weights, 1)
        kept, h = forward(x[0], *first)
        *terms1, by_h = middle(h, dy[0], *second)
        terms0 = last(x[0], by_h, kept, first[2])
        mine = [[summed(t) for t in terms0], [summed(t) for t in terms1]]
        gradients = [jnp.stack([mine[number][i] for number in range(2)]).astype(f32) for i in range(3)]
        squares = lax.psum(sum(jnp.sum(g * g) for g in gradients), "s")
        gradients = clipped(gradients, squares, lax.psum(1, "s") * sum(g.size for g in gradients))
        new = [adamw(w.astype(f32), m, v, g) for w, m, v, g in zip(weights, m, v, gradients, strict=True)]
        return tuple(one[which] for which in range(3) for one in new)

    states, cut = P(("rep", "r", "s"), None, None), P(None, "s", None)
    return jax.shard_map(
        step,
        mesh=mesh,
        in_specs=(states, states) + (cut,) * 9,
        out_specs=(P("rep", "s", None),) * 9,
        check_vma=False,
    )
```

time: 832 us -> 996 us (1.20)
  matrix products: 511 us -> 0 us
  Pallas kernels: 0 us -> 411 us
  waiting for transfers between devices: 216 us -> 526 us
  local copies, waits for them, and re-layouts: 33.7 us -> 7.07 us
  other arithmetic: 33.6 us -> 18.9 us
    dot_general x15 -> x0, matrix products: 511 us -> none  [the longest x5 186 us: layer(): up = jnp.dot(a, w['w_up'], preferred_element_type=jnp.float32)]
    pallas_call x0 -> x3, Pallas kernels: none -> 411 us  [call(): pl.pallas_call(kernel, out_shape=[jax.ShapeDtypeStruct(*o) for o in outs]...]
    reduce_scatter x6, waiting for transfers between devices: 99.5 us -> 297 us  [summed(): lax.psum_scatter(term, 's', scatter_dimension=0, tiled=True)]
    all_gather x6, waiting for transfers between devices: 23.4 us -> 134 us  [fetched(): return [lax.all_gather(w[number], 's', axis=0, tiled=True) for w in weights]]
    unnamed x40 -> x30, local copies, waits for them, and re-layouts: 26.8 us -> 2.52 us
  transfers between devices with their start and end apart: 13 -> 13, of which waited for: 7 -> 11; matrix products, arithmetic and copies ran while one was open for 48% -> 0% of each run, Pallas kernels for 0% -> 8%
where the time goes in v1:
time: 996 us; the launch traced here: 994 us
  waiting for transfers between devices  526 us (53%)
  Pallas kernels  411 us (41%)
  other arithmetic  18.9 us (2%)
  between operations  16.7 us (2%)
  blocking collectives  13.8 us (1%)
    pallas_call x3, Pallas kernels, call(): pl.pallas_call(kernel, out_shape=[jax.ShapeDtypeStruct(*o) for o in outs]...  411 us
    reduce_scatter x6, waiting for transfers between devices, summed(): lax.psum_scatter(term, 's', scatter_dimension=0, tiled=True)  297 us
    all_gather x6, waiting for transfers between devices, fetched(): return [lax.all_gather(w[number], 's', axis=0, tiled=True) for w in weights]  134 us
    psum x1, waiting for transfers between devices, summed(): lax.psum(lax.psum_scatter(term, 's', scatter_dimension=0, tiled=True), 'r')  91 us
  transfers between devices with their start and end apart: 13, of which 11 were waited for; matrix products, arithmetic and copies ran while one was open for 0% of the time, Pallas kernels for 8%

profile of v1, /device:TPU:0, one launch (start us, length us, event | category | flops | bytes accessed | tf_op | source)
XLA Modules:
  0.0 994.3 jit_solution(16487192252542308880)
XLA Ops:
  7.2 2.4 fusion.29
  9.7 1.1 fusion.28
  11.3 1.1 fusion.27
  14.2 33.3 %all-gather.13.cloned.1.call-done = bf16[1,896,2560]{2,1,0:T(8,128)(2,1)} async-done(((bf16[1,112,2560]{2,1,0:T(8,128)(2,1)}), bf16[1,896,2560]{2,1,0:T(8,128)(2,1)}) %all-gather.13.cloned.1.call-update) | async-done | bytes 4587536 | tf_op jit(solution)/shard_map/all_gather | solution.py:458
  47.5 36.7 %all-gather.15.cloned.1.call-done = bf16[1,896,2560]{2,1,0:T(8,128)(2,1)} async-done(((bf16[1,112,2560]{2,1,0:T(8,128)(2,1)}), bf16[1,896,2560]{2,1,0:T(8,128)(2,1)}) %all-gather.15.cloned.1.call-update) | async-done | bytes 4587536 | tf_op jit(solution)/shard_map/all_gather | solution.py:458
  84.1 36.7 %all-gather.17.cloned.1.call-done = bf16[1,2560,896]{2,1,0:T(8,128)(2,1)} async-done(((bf16[1,320,896]{2,1,0:T(8,128)(2,1)}), bf16[1,2560,896]{2,1,0:T(8,128)(2,1)}) %all-gather.17.cloned.1.call-update) | async-done | bytes 4587536 | tf_op jit(solution)/shard_map/all_gather | solution.py:458
  120.8 82.5 %shard_map.178 = (f32[10,4096,512]{2,1,0:T(8,128)}, bf16[4096,896]{1,0:T(8,128)(2,1)}) custom-call(bf16[4096,896]{1,0:T(8,128)(2,1)} %bitcast.14, bf16[896,2560]{1,0:T(8,128)(2,1)} %bitcast.22, bf16[896,2560]{1,0:T(8,128)(2,1)} %bitcast.23, bf16[2560,896]{1,0:T(8,128)(2,1)} %bitcast.16), custom_call_target="tpu_custom_call" | custom-call | tf_op jit(solution)/shard_map/pallas_call | solution.py:396
  203.3 27.0 %all-gather.23.cloned.1.call-done = bf16[1,2560,896]{2,1,0:T(8,128)(2,1)} async-done(((bf16[1,320,896]{2,1,0:T(8,128)(2,1)}), bf16[1,2560,896]{2,1,0:T(8,128)(2,1)}) %all-gather.23.cloned.1.call-update) | async-done | bytes 4587536 | tf_op jit(solution)/shard_map/all_gather | solution.py:458
  230.3 195.2 %shard_map.179 = (bf16[896,2560]{1,0:T(8,128)(2,1)}, bf16[896,2560]{1,0:T(8,128)(2,1)}, bf16[2560,896]{1,0:T(8,128)(2,1)}, bf16[4096,896]{1,0:T(8,128)(2,1)}) custom-call(bf16[4096,896]{1,0:T(8,128)(2,1)} %get-tuple-element.18.h_hbm, bf16[4096,896]{1,0:T(8,128)(2,1)} %bitcast.18, bf16[896,2560]{1,0:T(8,128)(2,1)} %bitcast.19, bf16[896,2560]{1,0:T(8,128)(2,1)} %bitcast.20, ...), custom_call_target="tpu_custom_call" | custom-call | tf_op jit(solution)/shard_map/pallas_call | solution.py:396
  425.5 133.7 %shard_map.180 = (bf16[896,2560]{1,0:T(8,128)(2,1)}, bf16[896,2560]{1,0:T(8,128)(2,1)}, bf16[2560,896]{1,0:T(8,128)(2,1)}) custom-call(bf16[4096,896]{1,0:T(8,128)(2,1)} %bitcast.15, bf16[4096,896]{1,0:T(8,128)(2,1)} %get-tuple-element.19.dy_hbm, f32[10,4096,512]{2,1,0:T(8,128)} %get-tuple-element.20.gu_hbm, bf16[2560,896]{1,0:T(8,128)(2,1)} %bitcast.17), custom_call_target="tpu_custom_call" | custom-call | tf_op jit(solution)/shard_map/pallas_call | solution.py:396
  562.7 43.8 %reduce-scatter.7.cloned.1.call-done = bf16[112,2560]{1,0:T(8,128)(2,1)} async-done(((bf16[896,2560]{1,0:T(8,128)(2,1)}), bf16[112,2560]{1,0:T(8,128)(2,1)}) %reduce-scatter.7.cloned.1.call-update) | async-done | bytes 573456 | tf_op jit(solution)/shard_map/reduce_scatter | solution.py:461
  606.5 50.6 %reduce-scatter.11.cloned.1.call-done = bf16[112,2560]{1,0:T(8,128)(2,1)} async-done(((bf16[896,2560]{1,0:T(8,128)(2,1)}), bf16[112,2560]{1,0:T(8,128)(2,1)}) %reduce-scatter.11.cloned.1.call-update) | async-done | bytes 573456 | tf_op jit(solution)/shard_map/reduce_scatter | solution.py:461
  657.1 50.6 %reduce-scatter.15.cloned.1.call-done = bf16[320,896]{1,0:T(8,128)(2,1)} async-done(((bf16[2560,896]{1,0:T(8,128)(2,1)}), bf16[320,896]{1,0:T(8,128)(2,1)}) %reduce-scatter.15.cloned.1.call-update) | async-done | bytes 573456 | tf_op jit(solution)/shard_map/reduce_scatter | solution.py:461
  707.7 50.5 %reduce-scatter.9.cloned.1.call-done = bf16[112,2560]{1,0:T(8,128)(2,1)} async-done(((bf16[896,2560]{1,0:T(8,128)(2,1)}), bf16[112,2560]{1,0:T(8,128)(2,1)}) %reduce-scatter.9.cloned.1.call-update) | async-done | bytes 573456 | tf_op jit(solution)/shard_map/reduce_scatter | solution.py:461
  758.2 50.6 %reduce-scatter.13.cloned.1.call-done = bf16[112,2560]{1,0:T(8,128)(2,1)} async-done(((bf16[896,2560]{1,0:T(8,128)(2,1)}), bf16[112,2560]{1,0:T(8,128)(2,1)}) %reduce-scatter.13.cloned.1.call-update) | async-done | bytes 573456 | tf_op jit(solution)/shard_map/reduce_scatter | solution.py:461
  808.8 50.5 %reduce-scatter.17.cloned.1.call-done = bf16[320,896]{1,0:T(8,128)(2,1)} async-done(((bf16[2560,896]{1,0:T(8,128)(2,1)}), bf16[320,896]{1,0:T(8,128)(2,1)}) %reduce-scatter.17.cloned.1.call-update) | async-done | bytes 573456 | tf_op jit(solution)/shard_map/reduce_scatter | solution.py:461
  859.3 91.0 %all-reduce.3.cloned.1.call-done = (bf16[1,112,2560]{2,1,0:T(8,128)(2,1)}, bf16[1,112,2560]{2,1,0:T(8,128)(2,1)}, bf16[1,112,2560]{2,1,0:T(8,128)(2,1)}, bf16[1,...) async-done(((bf16[1,112,2560]{2,1,0:T(8,128)(2,1)}, bf16[1,112,2560]{2,1,0:T(8,128)(2,1)}, bf16[1,112,2560]{2,1,0:T(8,128)(2,1)}, ...) | async-done | bytes 3440656 | tf_op jit(solution)/shard_map/psum | solution.py:461
  950.3 2.5 fusion.11
  952.8 2.4 fusion.10
  955.2 2.5 fusion.9
  959.7 13.8 %psum.55 = f32[]{:T(128)} all-reduce(f32[]{:T(128)S(6)} %add.75), channel_id=1, replica_groups=mesh['rep'=1,'r'=2,'s'=8] {'s'}, use_global_device_ids=true, to_apply=%region_15.0 | all-reduce | flops 1 | bytes 8 | tf_op jit(solution)/shard_map/psum | solution.py:471
  974.4 5.9 fusion.17
  980.2 1.1 copy-done.9
  982.3 5.5 fusion.8
  (57 shorter events, 6.7 us)
Async XLA Ops:
  7.2 40.3 %all-gather.13.cloned.1.call-start = ((), (), s32[]{:S(2)}) async-start(), calls=%async_computation.12 | async-start | bytes 5160960 | tf_op jit(solution)/shard_map/all_gather | solution.py:458
  9.7 74.5 %all-gather.15.cloned.1.call-start = ((), (), s32[]{:S(2)}) async-start(), calls=%async_computation.13 | async-start | bytes 5160960 | tf_op jit(solution)/shard_map/all_gather | solution.py:458
  10.8 110.0 %all-gather.17.cloned.1.call-start = ((), (), s32[]{:S(2)}) async-start(), calls=%async_computation.14 | async-start | bytes 5160960 | tf_op jit(solution)/shard_map/all_gather | solution.py:458
  12.4 190.9 %all-gather.19.cloned.1.call-start = ((), (), s32[]{:S(2)}) async-start(), calls=%async_computation.15 | async-start | bytes 5160960 | tf_op jit(solution)/shard_map/all_gather | solution.py:458
  13.0 190.3 %all-gather.21.cloned.1.call-start = ((), (), s32[]{:S(2)}) async-start(), calls=%async_computation.16 | async-start | bytes 5160960 | tf_op jit(solution)/shard_map/all_gather | solution.py:458
  13.6 216.8 %all-gather.23.cloned.1.call-start = ((), (), s32[]{:S(2)}) async-start(), calls=%async_computation.17 | async-start | bytes 5160960 | tf_op jit(solution)/shard_map/all_gather | solution.py:458
  14.2 592.4 %reduce-scatter.7.cloned.1.call-start = ((), (), s32[]{:S(2)}) async-start(), calls=%async_computation.6 | async-start | bytes 5160960 | tf_op jit(solution)/shard_map/reduce_scatter | solution.py:461
  559.3 97.8 %reduce-scatter.11.cloned.1.call-start = ((), (), s32[]{:S(2)}) async-start(), calls=%async_computation.8 | async-start | bytes 5160960 | tf_op jit(solution)/shard_map/reduce_scatter | solution.py:461
  560.0 147.7 %reduce-scatter.15.cloned.1.call-start = ((), (), s32[]{:S(2)}) async-start(), calls=%async_computation.10 | async-start | bytes 5160960 | tf_op jit(solution)/shard_map/reduce_scatter | solution.py:461
  560.8 197.4 %reduce-scatter.9.cloned.1.call-start = ((), (), s32[]{:S(2)}) async-start(), calls=%async_computation.7 | async-start | bytes 5160960 | tf_op jit(solution)/shard_map/reduce_scatter | solution.py:461
  561.3 247.4 %reduce-scatter.13.cloned.1.call-start = ((), (), s32[]{:S(2)}) async-start(), calls=%async_computation.9 | async-start | bytes 5160960 | tf_op jit(solution)/shard_map/reduce_scatter | solution.py:461
  562.1 297.2 %reduce-scatter.17.cloned.1.call-start = ((), (), s32[]{:S(2)}) async-start(), calls=%async_computation.11 | async-start | bytes 5160960 | tf_op jit(solution)/shard_map/reduce_scatter | solution.py:461
  562.7 387.6 %all-reduce.3.cloned.1.call-start = ((), (), s32[]{:S(2)}) async-start(), calls=%async_computation.18 | async-start | bytes 6881280 | tf_op jit(solution)/shard_map/psum | solution.py:461
  859.3 114.9 %copy-start.1 = (bf16[2,320,896]{2,1,0:T(8,128)(2,1)S(1)}, bf16[2,320,896]{2,1,0:T(8,128)(2,1)}, u32[]{:S(2)}) copy-start(bf16[2,320,896]{2,1,0:T(8,128)(2,1)} %param.15) | copy-start | bytes 3440644
  950.3 24.0 %copy-start.5 = (bf16[1,320,896]{2,1,0:T(8,128)(2,1)S(1)}, bf16[1,320,896]{2,1,0:T(8,128)(2,1)}, u32[]{:S(2)}) copy-start(bf16[1,320,896]{2,1,0:T(8,128)(2,1)} %get-tuple-element.31) | copy-start | bytes 1720324
  950.3 24.0 %copy-start.6 = (bf16[1,320,896]{2,1,0:T(8,128)(2,1)S(1)}, bf16[1,320,896]{2,1,0:T(8,128)(2,1)}, u32[]{:S(2)}) copy-start(bf16[1,320,896]{2,1,0:T(8,128)(2,1)} %get-tuple-element.32) | copy-start | bytes 1720324
  955.2 25.0 %copy-start.13 = (bf16[1,112,2560]{2,1,0:T(8,128)(2,1)S(1)}, bf16[1,112,2560]{2,1,0:T(8,128)(2,1)}, u32[]{:S(2)}) copy-start(bf16[1,112,2560]{2,1,0:T(8,128)(2,1)} %get-tuple-element.29) | copy-start | bytes 1720324
  955.2 25.0 %copy-start.14 = (bf16[1,112,2560]{2,1,0:T(8,128)(2,1)S(1)}, bf16[1,112,2560]{2,1,0:T(8,128)(2,1)}, u32[]{:S(2)}) copy-start(bf16[1,112,2560]{2,1,0:T(8,128)(2,1)} %get-tuple-element.30) | copy-start | bytes 1720324
  974.3 6.0 copy-start.2
  974.3 5.9 copy-start.4
  974.3 7.1 copy-start.9
  974.3 7.7 copy-start.10
  974.3 7.8 copy-start.11
  974.3 7.9 copy-start.12
  (4 other events, 16.1 us)
Sparse Core Ops, SparseCore 0:
  10.4 37.0 all-gather.12
  49.9 34.1 all-gather.14
  86.5 34.1 all-gather.16
  123.1 34.2 all-gather.18
  159.6 34.2 all-gather.20
  196.1 34.1 all-gather.22
  559.4 47.0 reduce-scatter.6
  610.0 47.1 reduce-scatter.10
  660.6 47.1 reduce-scatter.14
  711.0 47.1 reduce-scatter.8
  761.6 47.1 reduce-scatter.12
  812.1 47.1 reduce-scatter.16
  862.0 88.2 all-reduce.2

commit v2 on v1

--- a/solution.py
+++ b/solution.py
@@ -13,6 +13,7 @@
 NT_DIMS = (((1,), (1,)), ((), ()))
 TN_DIMS = (((0,), (0,)), ((), ()))
 VMEM_LIMIT = 67043328
+MESH = pl.DeviceIdType.MESH
 
 
 def groups_of(i):
@@ -166,10 +167,351 @@
         wait(outputs(t))
 
 
-def middle_kernel(h_hbm, dy_hbm, wg_hbm, wu_hbm, wd_hbm, dwg_hbm, dwu_hbm, dwd_hbm, dh_hbm,
-                  a_ref, aT_ref, dy_ref, da_ref, dgu_ref, act_ref, wgu, wd, ob, obd, hsem, ysem, wsem, osem):
+def when(condition):
+    if isinstance(condition, bool):
+        return (lambda f: f()) if condition else (lambda f: None)
+    return pl.when(condition)
+
+
+class Place:
+    def __init__(self):
+        s = lax.axis_index("s")
+        self.c, self.y, self.x = s % 2, (s // 2) % 2, s // 4
+        self.core = {"s": s + 1 - 2 * self.c}
+        self.over_y = {"s": s + 2 - 4 * self.y}
+        self.over_x = {"s": s + 4 - 8 * self.x}
+        self.over_z = {"r": 1 - lax.axis_index("r")}
+
+    def barrier(self):
+        barrier = pltpu.get_barrier_semaphore()
+        for device in (self.core, self.over_y, self.over_x, self.over_z):
+            pl.semaphore_signal(barrier, inc=1, device_id=device, device_id_type=MESH)
+        pl.semaphore_wait(barrier, 4)
+
+
+def remote(source, target, send, receive, device):
+    return pltpu.make_async_remote_copy(source, target, send, receive, device_id=device, device_id_type=MESH)
+
+
+def give(semaphore, device):
+    pl.semaphore_signal(semaphore, inc=1, device_id=device, device_id_type=MESH)
+
+
+class Reducer:
+    SHAPES = (((2, 4, 2), bf16), ((4, 2), bf16), ((2, 2), bf16), ((2, 2), f32), ((2, 2), bf16), ((2,), bf16), ((2,), f32), ((2,), bf16), ((2,), bf16), ((2,), bf16), ((2,), bf16))
+
+    @classmethod
+    def scratch(cls, slots, block):
+        D, R = pltpu.SemaphoreType.DMA, pltpu.SemaphoreType.REGULAR
+        buffers = [pltpu.VMEM((slots,) + lead + block, kind) for lead, kind in cls.SHAPES]
+        return buffers + [D((2, slots)), D((2, slots, 2)), D((2, slots, 2)), D((2, slots)), R((slots,)), R((slots, 2)), R((slots, 2)), R((slots,)), pltpu.VMEM((8, block[1]), f32)]
+
+    COUNT = 20
+
+    def __init__(self, place, refs):
+        self.place = place
+        self.all, self.got0, self.out1, self.kept1, self.got1, self.out2, self.kept2, self.got2, self.out3, self.got3, self.out = refs[:11]
+        self.sem0, self.sem1, self.sem2, self.sem3, self.free0, self.free1, self.free2, self.free3, self.squares = refs[11:]
+        self.squares[...] = jnp.zeros_like(self.squares)
+        self.first_way, self.second_way = (place.over_x, place.over_y), (place.over_y, place.over_x)
+
+    def copy0(self, b):
+        return remote(self.all.at[b, 1 - self.place.c], self.got0.at[b], self.sem0.at[0, b], self.sem0.at[1, b], self.place.core)
+
+    def copy1(self, b, p):
+        return remote(self.out1.at[b, p], self.got1.at[b, p], self.sem1.at[0, b, p], self.sem1.at[1, b, p], self.first_way[p])
+
+    def copy2(self, b, p):
+        return remote(self.out2.at[b, p], self.got2.at[b, p], self.sem2.at[0, b, p], self.sem2.at[1, b, p], self.second_way[p])
+
+    def copy3(self, b):
+        return remote(self.out3.at[b], self.got3.at[b], self.sem3.at[0, b], self.sem3.at[1, b], self.place.over_z)
+
+    def send(self, b, first):
+        @when(not first if isinstance(first, bool) else jnp.logical_not(first))
+        def _():
+            pl.semaphore_wait(self.free0.at[b], 1)
+
+        self.copy0(b).start()
+
+    def after_core(self, b, first, final):
+        place, c = self.place, self.place.c
+        self.copy0(b).wait()
+        for p in range(2):
+            for n in range(2):
+                away, near = ((1 - place.x) * 2 + n, place.x * 2 + n) if p == 0 else (n * 2 + 1 - place.y, n * 2 + place.y)
+                self.out1[b, p, n] = (self.all[b, c, away, p].astype(f32) + self.got0[b, away, p].astype(f32)).astype(bf16)
+                self.kept1[b, p, n] = self.all[b, c, near, p].astype(f32) + self.got0[b, near, p].astype(f32)
+
+        @when(not final if isinstance(final, bool) else jnp.logical_not(final))
+        def _():
+            give(self.free0.at[b], place.core)
+
+        @when(not first if isinstance(first, bool) else jnp.logical_not(first))
+        def _():
+            for p in range(2):
+                pl.semaphore_wait(self.free1.at[b, p], 1)
+
+        for p in range(2):
+            self.copy1(b, p).start()
+
+    def after_first(self, b, first, final):
+        place = self.place
+        for p in range(2):
+            self.copy1(b, p).wait()
+            near = place.y if p == 0 else place.x
+            self.out2[b, p] = (self.kept1[b, p, 1 - near] + self.got1[b, p, 1 - near].astype(f32)).astype(bf16)
+            self.kept2[b, p] = self.kept1[b, p, near] + self.got1[b, p, near].astype(f32)
+
+        @when(not final if isinstance(final, bool) else jnp.logical_not(final))
+        def _():
+            for p in range(2):
+                give(self.free1.at[b, p], self.first_way[p])
+
+        @when(not first if isinstance(first, bool) else jnp.logical_not(first))
+        def _():
+            for p in range(2):
+                pl.semaphore_wait(self.free2.at[b, p], 1)
+
+        for p in range(2):
+            self.copy2(b, p).start()
+
+    def after_second(self, b, first, final):
+        for p in range(2):
+            self.copy2(b, p).wait()
+            self.out3[b, p] = (self.kept2[b, p] + self.got2[b, p].astype(f32)).astype(bf16)
+
+        @when(not final if isinstance(final, bool) else jnp.logical_not(final))
+        def _():
+            for p in range(2):
+                give(self.free2.at[b, p], self.second_way[p])
+
+        @when(not first if isinstance(first, bool) else jnp.logical_not(first))
+        def _():
+            pl.semaphore_wait(self.free3.at[b], 1)
+
+        self.copy3(b).start()
+
+    def after_copy(self, b, final):
+        self.copy3(b).wait()
+        for p in range(2):
+            g = (self.out3[b, p].astype(f32) + self.got3[b, p].astype(f32)).astype(bf16)
+            self.out[b, p] = g
+            g = g.astype(f32)
+            self.squares[...] += jnp.sum((g * g).reshape(g.shape[0] // 8, 8, g.shape[1]), 0)
+
+        @when(not final if isinstance(final, bool) else jnp.logical_not(final))
+        def _():
+            give(self.free3.at[b], self.place.over_z)
+
+
+class Gradients:
+    @staticmethod
+    def scratch(rows, down_rows, D):
+        V, S = pltpu.VMEM, pltpu.SemaphoreType.DMA
+        return (
+            Reducer.scratch(2, (rows, CH)) + Reducer.scratch(1, (32, D))
+            + [V((5, 64, D), bf16), S((2, 2, 2)), S((5,)), S((2, 2))]
+        )
+
+    def __init__(self, place, refs, outs, NC):
+        n = Reducer.COUNT
+        self.place, self.NC = place, NC
+        self.wide = Reducer(place, refs[:n])
+        self.down = Reducer(place, refs[n : 2 * n])
+        self.down_out, self.out_sem, self.local_sem, self.cross_sem = refs[2 * n :]
+        self.gate_hbm, self.up_hbm, self.down_hbm = outs
+
+    def flags(self, i):
+        b = i % 2
+        return b, i < 2, i + 2 >= self.NC
+
+    def put_wide(self, i, value):
+        b, rows = i % 2, value.shape[0] // 8
+        value = value.astype(bf16)
+        for s in range(8):
+            for p in range(2):
+                self.wide.all[b, s % 2, s // 2, p] = value[rows * s : rows * (s + 1), CH * p : CH * (p + 1)]
+
+    def put_down(self, i, value):
+        half = i % 2
+        value = value.astype(bf16)
+        for n in range(2):
+            for core in range(2):
+                for p in range(2):
+                    at = LANES * n + 64 * core + 32 * p
+                    self.down.all[0, core, 2 * half + n, p] = value[at : at + 32]
+
+    def wide_send(self, i):
+        b, first, _ = self.flags(i)
+        self.wide.send(b, first)
+
+    def wide1(self, i):
+        self.wide.after_core(*self.flags(i))
+
+    def wide2(self, i):
+        self.wide.after_first(*self.flags(i))
+
+    def wide3(self, i):
+        self.wide.after_second(*self.flags(i))
+
+    def wide_outs(self, i):
+        b = i % 2
+        return [
+            pltpu.make_async_copy(
+                self.wide.out.at[b, p, :, pl.ds(LANES * n, LANES)], (self.gate_hbm, self.up_hbm)[p].at[:, rows_at(at, LANES)], self.out_sem.at[b, p, n]
+            )
+            for p in range(2)
+            for n, at in enumerate(groups_of(i))
+        ]
+
+    def wide4(self, i):
+        b, first, final = self.flags(i)
+
+        @when(not first if isinstance(first, bool) else jnp.logical_not(first))
+        def _():
+            wait(self.wide_outs(i - 2))
+
+        self.wide.after_copy(b, final)
+        start(self.wide_outs(i))
+
+    def rounds(self, j):
+        return 0, j < 1, j >= self.NC // 2 - 1
+
+    def down_send(self, j):
+        self.down.send(0, j < 1)
+
+    def down1(self, j):
+        self.down.after_core(*self.rounds(j))
+
+    def down2(self, j):
+        self.down.after_first(*self.rounds(j))
+
+    def down3(self, j):
+        self.down.after_second(*self.rounds(j))
+
+    def down_rows(self, j):
+        unit = 2 * j + self.place.c
+        return rows_at((unit % 5) * 64, 64), unit // 5 == self.place.c
+
+    def down_local(self, j):
+        rows, _ = self.down_rows(j)
+        return pltpu.make_async_copy(self.down_out.at[j], self.down_hbm.at[rows, :], self.local_sem.at[j])
+
+    def down_cross(self, j):
+        rows, _ = self.down_rows(j)
+        return remote(self.down_out.at[j], self.down_hbm.at[rows, :], self.cross_sem.at[0, j % 3], self.cross_sem.at[1, j % 3], self.place.core)
+
+    def down4(self, j):
+        self.down.after_copy(0, self.rounds(j)[2])
+        for p in range(2):
+            self.down_out[j, pl.ds(32 * p, 32), :] = self.down.out[0, p]
+        _, mine = self.down_rows(j)
+
+        @pl.when(mine)
+        def _():
+            self.down_local(j).start()
+
+        @pl.when(jnp.logical_not(mine))
+        def _():
+            self.down_cross(j).start()
+
+    def in_tiles(self, i):
+        @when(i >= 1)
+        def _():
+            self.wide1(i - 1)
+
+        @when(i >= 3)
+        def _():
+            self.wide4(i - 3)
+
+    def after_down(self, i):
+        j = i // 2
+
+        @when(i % 2 == 1)
+        def _():
+            @when(i >= 3)
+            def _():
+                self.down4(j - 1)
+
+            self.down_send(j)
+
+        @when(jnp.logical_and(i % 2 == 0, i >= 2))
+        def _():
+            self.down2(j - 1)
+
+        @when(i >= 2)
+        def _():
+            self.wide3(i - 2)
+
+    def after_wide(self, i):
+        j = i // 2
+        self.wide_send(i)
+
+        @when(i >= 1)
+        def _():
+            self.wide2(i - 1)
+
+        @when(i % 2 == 1)
+        def _():
+            self.down1(j)
+
+        @when(jnp.logical_and(i % 2 == 0, i >= 2))
+        def _():
+            self.down3(j - 1)
+
+    def tail(self):
+        n, j = self.NC, self.NC // 2 - 1
+
+        def first():
+            self.wide4(n - 3)
+            self.wide3(n - 2)
+            self.down2(j)
+            self.wide1(n - 1)
+
+        def second():
+            self.down3(j)
+            self.wide4(n - 2)
+            self.wide2(n - 1)
+
+        def third():
+            self.down4(j)
+            self.wide3(n - 1)
+
+        def fourth():
+            self.wide4(n - 1)
+
+        return first, second, third, fourth
+
+    def squares(self):
+        total = jnp.zeros((8, LANES), f32)
+        for ref in (self.wide.squares, self.down.squares):
+            for n in range(ref.shape[1] // LANES):
+                total += ref[:, pl.ds(LANES * n, LANES)]
+        return total
+
+    def finish(self):
+        for i in (self.NC - 2, self.NC - 1):
+            wait(self.wide_outs(i))
+        for j in range(5):
+            _, mine = self.down_rows(j)
+
+            @pl.when(mine)
+            def _():
+                self.down_local(j).wait()
+
+            @pl.when(jnp.logical_not(mine))
+            def _():
+                self.down_cross(j).wait_send()
+
+        for n in range(2):
+            self.down_cross(n).wait_recv()
+
+
+def middle_kernel(h_hbm, dy_hbm, wg_hbm, wu_hbm, wd_hbm, gg_hbm, gu_hbm, gd_hbm, dh_hbm, sq_hbm,
+                  a_ref, aT_ref, dy_ref, da_ref, dgu_ref, act_ref, wgu, wd, sq, hsem, ysem, wsem, qsem, *refs):
     T, D = a_ref.shape
-    F = dwg_hbm.shape[1]
+    F = wg_hbm.shape[1]
     NC, NT = F // CH, T // TM
 
     def loads(t):
@@ -187,21 +529,12 @@
             + rows_in(wd_hbm, wd.at[slot], wsem.at[slot, 2], i)
         )
 
-    def outs(i):
-        slot = i % 2
-        copies = []
-        for n, at in enumerate(groups_of(i)):
-            cols = rows_at(at, LANES)
-            copies += [
-                pltpu.make_async_copy(ob.at[slot, :, pl.ds(LANES * n, LANES)], dwg_hbm.at[:, cols], osem.at[slot, 0, n]),
-                pltpu.make_async_copy(ob.at[slot, :, pl.ds(CH + LANES * n, LANES)], dwu_hbm.at[:, cols], osem.at[slot, 1, n]),
-                pltpu.make_async_copy(obd.at[slot, pl.ds(LANES * n, LANES), :], dwd_hbm.at[cols, :], osem.at[slot, 2, n]),
-            ]
-        return copies
-
     lax.fori_loop(0, T // 256, lambda t, _: start(loads(t)) or 0, 0)
     start(weights(0))
     start(dys())
+    place = Place()
+    gradients = Gradients(place, refs, (gg_hbm, gu_hbm, gd_hbm), NC)
+    place.barrier()
 
     def norm(t, _):
         wait(loads(t))
@@ -221,6 +554,10 @@
             start(weights(i + 1))
 
         def tile(t, _):
+            @pl.when(t == 2)
+            def _():
+                gradients.in_tiles(i)
+
             def rows_of(k):
                 return rows_at(t * TM + k * SUB, SUB)
 
@@ -256,13 +593,10 @@
 
         lax.fori_loop(0, NT, tile, 0)
 
-        @pl.when(i >= 2)
-        def _():
-            wait(outs(i - 2))
-
-        ob[slot] = dot(aT_ref[...], dgu_ref[...]).astype(bf16)
-        obd[slot] = lax.dot_general(act_ref[...], dy_ref[...], TN_DIMS, preferred_element_type=f32).astype(bf16)
-        start(outs(i))
+        gradients.put_down(i, lax.dot_general(act_ref[...], dy_ref[...], TN_DIMS, preferred_element_type=f32))
+        gradients.after_down(i)
+        gradients.put_wide(i, dot(aT_ref[...], dgu_ref[...]))
+        gradients.after_wide(i)
         return 0
 
     lax.fori_loop(0, NC, chunk, 0)
@@ -282,18 +616,26 @@
         by_h = (da * scale - w * along).astype(bf16)
         dy_ref[rows, :] = (dy_ref[rows, :].astype(f32) + by_h.astype(f32)).astype(bf16)
         start(stores(t))
+        for at, step in ((T // 512 - 2, second), (T // 256 - 5, third)):
+            pl.when(t == at)(step)
         return 0
 
+    first, second, third, fourth = gradients.tail()
+    first()
     lax.fori_loop(0, T // 256, norm_back, 0)
+    fourth()
+    sq[...] = gradients.squares()
+    done = pltpu.make_async_copy(sq, sq_hbm, qsem)
+    done.start()
     lax.fori_loop(0, T // 256, lambda t, _: wait(stores(t)) or 0, 0)
-    for i in (NC - 2, NC - 1):
-        wait(outs(i))
-
-
-def last_kernel(h_hbm, dy_hbm, gu_hbm, wd_hbm, dwg_hbm, dwu_hbm, dwd_hbm,
-                a_ref, aT_ref, dy_ref, dgu_ref, act_ref, gus, wd, ob, obd, hsem, ysem, gsem, wsem, osem):
+    gradients.finish()
+    done.wait()
+
+
+def last_kernel(h_hbm, dy_hbm, kept_hbm, wd_hbm, sq_in, gg_hbm, gu_hbm, gd_hbm, sq_hbm,
+                a_ref, aT_ref, dy_ref, dgu_ref, act_ref, gus, wd, sq, parts, hsem, ysem, gsem, wsem, qsem, psem, *refs):
     T, D = a_ref.shape
-    F = dwg_hbm.shape[1]
+    F = wd_hbm.shape[0]
     NC, NT = F // CH, T // TM
 
     def loads(t):
@@ -309,24 +651,18 @@
 
     def kept(n):
         i, t = n // NT, n % NT
-        return [pltpu.make_async_copy(gu_hbm.at[i, rows_at(t * TM, TM), :], gus.at[n % 2], gsem.at[n % 2])]
-
-    def outs(i):
-        slot = i % 2
-        copies = []
-        for n, at in enumerate(groups_of(i)):
-            cols = rows_at(at, LANES)
-            copies += [
-                pltpu.make_async_copy(ob.at[slot, :, pl.ds(LANES * n, LANES)], dwg_hbm.at[:, cols], osem.at[slot, 0, n]),
-                pltpu.make_async_copy(ob.at[slot, :, pl.ds(CH + LANES * n, LANES)], dwu_hbm.at[:, cols], osem.at[slot, 1, n]),
-                pltpu.make_async_copy(obd.at[slot, pl.ds(LANES * n, LANES), :], dwd_hbm.at[cols, :], osem.at[slot, 2, n]),
-            ]
-        return copies
+        return [pltpu.make_async_copy(kept_hbm.at[i, rows_at(t * TM, TM), :], gus.at[n % NT], gsem.at[n % NT])]
 
     lax.fori_loop(0, T // 256, lambda t, _: start(loads(t)) or 0, 0)
     start(weights(0))
     start(dys())
-    start(kept(0))
+    for n in range(NT):
+        start(kept(n))
+    before = pltpu.make_async_copy(sq_in, sq, qsem)
+    before.start()
+    place = Place()
+    gradients = Gradients(place, refs, (gg_hbm, gu_hbm, gd_hbm), NC)
+    place.barrier()
 
     def norm(t, _):
         wait(loads(t))
@@ -348,9 +684,9 @@
             n = i * NT + t
             wait(kept(n))
 
-            @pl.when(n + 1 < NC * NT)
+            @pl.when(t == 2)
             def _():
-                start(kept(n + 1))
+                gradients.in_tiles(i)
 
             def rows_of(k):
                 return rows_at(t * TM + k * SUB, SUB)
@@ -361,7 +697,7 @@
             def elementwise(k, dact):
                 rows = rows_of(k)
                 dact = dact.astype(bf16).astype(f32)
-                gate, up = gus[n % 2, pl.ds(k * SUB, SUB), pl.ds(0, CH)], gus[n % 2, pl.ds(k * SUB, SUB), pl.ds(CH, CH)]
+                gate, up = gus[t, pl.ds(k * SUB, SUB), pl.ds(0, CH)], gus[t, pl.ds(k * SUB, SUB), pl.ds(CH, CH)]
                 sg = sigmoid(gate)
                 silu = gate * sg
                 act_ref[rows, :] = (silu * up).astype(bf16)
@@ -373,22 +709,36 @@
                 following = dots(k + 1) if k + 1 < TM // SUB else None
                 elementwise(k, now)
                 now = following
+
+            @pl.when(n + NT < NC * NT)
+            def _():
+                start(kept(n + NT))
+
             return 0
 
         lax.fori_loop(0, NT, tile, 0)
 
-        @pl.when(i >= 2)
-        def _():
-            wait(outs(i - 2))
-
-        ob[slot] = dot(aT_ref[...], dgu_ref[...]).astype(bf16)
-        obd[slot] = lax.dot_general(act_ref[...], dy_ref[...], TN_DIMS, preferred_element_type=f32).astype(bf16)
-        start(outs(i))
+        gradients.put_down(i, lax.dot_general(act_ref[...], dy_ref[...], TN_DIMS, preferred_element_type=f32))
+        gradients.after_down(i)
+        gradients.put_wide(i, dot(aT_ref[...], dgu_ref[...]))
+        gradients.after_wide(i)
         return 0
 
     lax.fori_loop(0, NC, chunk, 0)
-    for i in (NC - 2, NC - 1):
-        wait(outs(i))
+    before.wait()
+    for step in gradients.tail():
+        step()
+    sq[...] += gradients.squares()
+    for n, device in enumerate((place.core, place.over_y, place.over_x)):
+        parts[0, n] = sq[...]
+        exchange = remote(parts.at[0, n], parts.at[1, n], psem.at[0, n], psem.at[1, n], device)
+        exchange.start()
+        exchange.wait()
+        sq[...] += parts[1, n]
+    done = pltpu.make_async_copy(sq, sq_hbm, qsem)
+    done.start()
+    gradients.finish()
+    done.wait()
 
 
 def call(kernel, outs, scratch, inputs, **params):
@@ -420,24 +770,30 @@
     V, S = pltpu.VMEM, pltpu.SemaphoreType.DMA
     return call(
         middle_kernel,
-        [((D, F), bf16), ((D, F), bf16), ((F, D), bf16), ((T, D), bf16)],
+        [((D // 8, F), bf16), ((D // 8, F), bf16), ((F // 8, D), bf16), ((T, D), bf16), ((8, LANES), f32)],
         [V((T, D), bf16), V((D, T), bf16), V((T, D), bf16), V((T, D), f32), V((T, 2 * CH), bf16), V((T, CH), bf16)]
-        + [V((2, D, 2 * CH), bf16), V((2, CH, D), bf16), V((2, D, 2 * CH), bf16), V((2, CH, D), bf16)]
-        + [S((T // 256,)), S(()), S((2, 3, 2)), S((2, 3, 2))],
+        + [V((2, D, 2 * CH), bf16), V((2, CH, D), bf16), V((8, LANES), f32)]
+        + [S((T // 256,)), S(()), S((2, 3, 2)), S(())]
+        + Gradients.scratch(D // 8, F // 8, D),
         (h, dy, wg, wu, wd),
+        collective_id=1,
+        has_side_effects=True,
     )
 
 
-def last(h, dy, gu, wd):
+def last(h, dy, gu, wd, squares):
     (T, D), F = h.shape, wd.shape[0]
     V, S = pltpu.VMEM, pltpu.SemaphoreType.DMA
     return call(
         last_kernel,
-        [((D, F), bf16), ((D, F), bf16), ((F, D), bf16)],
-        [V((T, D), bf16), V((D, T), bf16), V((T, D), bf16), V((T, 2 * CH), bf16), V((T, CH), bf16), V((2, TM, 2 * CH), f32)]
-        + [V((2, CH, D), bf16), V((2, D, 2 * CH), bf16), V((2, CH, D), bf16)]
-        + [S((T // 256,)), S(()), S((2,)), S((2, 2)), S((2, 3, 2))],
-        (h, dy, gu, wd),
+        [((D // 8, F), bf16), ((D // 8, F), bf16), ((F // 8, D), bf16), ((8, LANES), f32)],
+        [V((T, D), bf16), V((D, T), bf16), V((T, D), bf16), V((T, 2 * CH), bf16), V((T, CH), bf16), V((T // TM, TM, 2 * CH), f32)]
+        + [V((2, CH, D), bf16), V((8, LANES), f32), V((2, 3, 8, LANES), f32)]
+        + [S((T // 256,)), S(()), S((T // TM,)), S((2, 2)), S(()), S((2, 3))]
+        + Gradients.scratch(D // 8, F // 8, D),
+        (h, dy, gu, wd, squares),
+        collective_id=2,
+        has_side_effects=True,
     )
 
 
@@ -457,19 +813,14 @@
     def fetched(weights, number):
         return [lax.all_gather(w[number], "s", axis=0, tiled=True) for w in weights]
 
-    def summed(term):
-        return lax.psum(lax.psum_scatter(term, "s", scatter_dimension=0, tiled=True), "r")
-
     def step(x, dy, *arrays):
         weights, m, v = (arrays[i : i + 3] for i in (0, 3, 6))
         first, second = fetched(weights, 0), fetched(weights, 1)
         kept, h = forward(x[0], *first)
-        *terms1, by_h = middle(h, dy[0], *second)
-        terms0 = last(x[0], by_h, kept, first[2])
-        mine = [[summed(t) for t in terms0], [summed(t) for t in terms1]]
-        gradients = [jnp.stack([mine[number][i] for number in range(2)]).astype(f32) for i in range(3)]
-        squares = lax.psum(sum(jnp.sum(g * g) for g in gradients), "s")
-        gradients = clipped(gradients, squares, lax.psum(1, "s") * sum(g.size for g in gradients))
+        *second_sums, by_h, squares = middle(h, dy[0], *second)
+        *first_sums, squares = last(x[0], by_h, kept, first[2], squares)
+        gradients = [jnp.stack(pair).astype(f32) for pair in zip(first_sums, second_sums, strict=True)]
+        gradients = clipped(gradients, jnp.sum(squares), lax.psum(1, "s") * sum(g.size for g in gradients))
         new = [adamw(w.astype(f32), m, v, g) for w, m, v, g in zip(weights, m, v, gradients, strict=True)]
         return tuple(one[which] for which in range(3) for one in new)
 

time: 996 us -> 615 us (0.62)
  waiting for transfers between devices: 526 us -> 135 us
  Pallas kernels: 411 us -> 443 us
  blocking collectives: 13.8 us -> 0 us
    reduce_scatter x6 -> x0, waiting for transfers between devices: 297 us -> none  [summed(): lax.psum_scatter(term, 's', scatter_dimension=0, tiled=True)]
    psum x1 -> x0, waiting for transfers between devices: 91 us -> none  [summed(): lax.psum(lax.psum_scatter(term, 's', scatter_dimension=0, tiled=True), 'r')]
    pallas_call x3, Pallas kernels: 411 us -> 443 us  [call(): pl.pallas_call(kernel, out_shape=[jax.ShapeDtypeStruct(*o) for o in outs]...]
    psum x1 -> x0, blocking collectives: 13.8 us -> none  [step(): squares = lax.psum(sum((jnp.sum(g * g) for g in gradients)), 's')]
  transfers between devices with their start and end apart: 13 -> 6, of which waited for: 11 -> 4; matrix products, arithmetic and copies ran while one was open for 0% -> 0% of each run, Pallas kernels for 8% -> 13%
where the time goes in v2:
time: 615 us
  Pallas kernels  443 us (72%)
  waiting for transfers between devices  135 us (22%)
  between operations  14.9 us (2%)
  other arithmetic  14.4 us (2%)
  local copies, waits for them, and re-layouts  7.03 us (1%)
    pallas_call x3, Pallas kernels, call(): pl.pallas_call(kernel, out_shape=[jax.ShapeDtypeStruct(*o) for o in outs]...  443 us
    all_gather x6, waiting for transfers between devices, fetched(): return [lax.all_gather(w[number], 's', axis=0, tiled=True) for w in weights]  134 us
    convert_element_type x2, other arithmetic, adamw(): return ((w - 0.02 * step).astype(bf16), m, v)  13.1 us
  transfers between devices with their start and end apart: 6, of which 4 were waited for; matrix products, arithmetic and copies ran while one was open for 0% of the time, Pallas kernels for 13%

profile of v2, /device:TPU:0, one launch (start us, length us, event | category | flops | bytes accessed | tf_op | source)
XLA Modules:
  0.0 614.7 jit_solution(16827592221580725842)
XLA Ops:
  7.2 2.4 fusion.15
  9.7 0.0 all-gather.13.cloned.1.call-start
  9.7 1.1 fusion.17
  10.8 0.0 all-gather.15.cloned.1.call-start
  10.9 0.4 copy-done.2
  11.3 1.1 fusion.16
  12.4 0.0 all-gather.19.cloned.1.call-start
  12.5 0.5 all-gather.19.cloned.1.call-update
  13.0 0.5 all-gather.21.cloned.1.call-update
  13.6 0.5 all-gather.23.cloned.1.call-update
  14.2 33.3 %all-gather.17.cloned.1.call-done = bf16[1,2560,896]{2,1,0:T(8,128)(2,1)} async-done(((bf16[1,320,896]{2,1,0:T(8,128)(2,1)}), bf16[1,2560,896]{2,1,0:T(8,128)(2,1)}) %all-gather.17.cloned.1.call-update) | async-done | bytes 4587536 | tf_op jit(solution)/shard_map/all_gather | solution.py:814
  47.5 36.7 %all-gather.13.cloned.1.call-done = bf16[1,896,2560]{2,1,0:T(8,128)(2,1)} async-done(((bf16[1,112,2560]{2,1,0:T(8,128)(2,1)}), bf16[1,896,2560]{2,1,0:T(8,128)(2,1)}) %all-gather.13.cloned.1.call-update) | async-done | bytes 4587536 | tf_op jit(solution)/shard_map/all_gather | solution.py:814
  84.1 36.7 %all-gather.15.cloned.1.call-done = bf16[1,896,2560]{2,1,0:T(8,128)(2,1)} async-done(((bf16[1,112,2560]{2,1,0:T(8,128)(2,1)}), bf16[1,896,2560]{2,1,0:T(8,128)(2,1)}) %all-gather.15.cloned.1.call-update) | async-done | bytes 4587536 | tf_op jit(solution)/shard_map/all_gather | solution.py:814
  120.8 82.6 %shard_map.178 = (f32[10,4096,512]{2,1,0:T(8,128)}, bf16[4096,896]{1,0:T(8,128)(2,1)}) custom-call(bf16[4096,896]{1,0:T(8,128)(2,1)} %bitcast.14, bf16[896,2560]{1,0:T(8,128)(2,1)} %bitcast.22, bf16[896,2560]{1,0:T(8,128)(2,1)} %bitcast.23, bf16[2560,896]{1,0:T(8,128)(2,1)} %bitcast.16), custom_call_target="tpu_custom_call" | custom-call | tf_op jit(solution)/shard_map/pallas_call | solution.py:746
  203.4 27.0 %all-gather.23.cloned.1.call-done = bf16[1,2560,896]{2,1,0:T(8,128)(2,1)} async-done(((bf16[1,320,896]{2,1,0:T(8,128)(2,1)}), bf16[1,2560,896]{2,1,0:T(8,128)(2,1)}) %all-gather.23.cloned.1.call-update) | async-done | bytes 4587536 | tf_op jit(solution)/shard_map/all_gather | solution.py:814
  230.4 212.8 %shard_map.179 = (bf16[112,2560]{1,0:T(8,128)(2,1)}, bf16[112,2560]{1,0:T(8,128)(2,1)}, bf16[320,896]{1,0:T(8,128)(2,1)}, bf16[4096,896]{1,0:T(8,128)(2,1)}, f32[8,128]{1,0:T(8,128)}) custom-call(bf16[4096,896]{1,0:T(8,128)(2,1)} %get-tuple-element.20.h_hbm, bf16[4096,896]{1,0:T(8,128)(2,1)} %bitcast.18, bf16[896,2560]{1,0:T(8,128)(2,1)} %bitcast.19, ...), custom_call_target="tpu_custom_call" | custom-call | tf_op jit(solution)/shard_map/pallas_call | solution.py:746
  443.2 147.4 %shard_map.180 = (bf16[112,2560]{1,0:T(8,128)(2,1)}, bf16[112,2560]{1,0:T(8,128)(2,1)}, bf16[320,896]{1,0:T(8,128)(2,1)}, f32[8,128]{1,0:T(8,128)}) custom-call(bf16[4096,896]{1,0:T(8,128)(2,1)} %bitcast.15, bf16[4096,896]{1,0:T(8,128)(2,1)} %get-tuple-element.21.dy_hbm, f32[10,4096,512]{2,1,0:T(8,128)} %get-tuple-element.22.kept_hbm, ...), custom_call_target="tpu_custom_call" | custom-call | tf_op jit(solution)/shard_map/pallas_call | solution.py:746
  590.6 1.3 reduce_sum.9
  592.7 6.5 %fusion.8 = (bf16[2,320,896]{2,1,0:T(8,128)(2,1)}, f32[2,320,896]{2,1,0:T(8,128)}, f32[2,320,896]{2,1,0:T(8,128)}) fusion(bf16[2,320,896]{2,1,0:T(8,128)(2,1)} %param.15, f32[]{:T(128)S(6)} %min_shard_map.3, bf16[1,320,896]{2,1,0:T(8,128)(2,1)} %bitcast.24, bf16[1,320,896]{2,1,0:T(8,128)(2,1)} %bitcast.25, f32[2,320,896]{2,1,0:T(8,128)} %param.21, ...), kind=kLoop, calls=%fused_computation.17 | loop fusion | flops 11468800 | bytes 12615684 | tf_op jit(solution)/shard_map/convert_element_type | solution.py:804
  599.3 1.1 copy-done.6
  600.4 0.7 copy-done.7
  601.0 0.0 copy-done.8
  601.1 0.2 copy-done.9
  601.2 6.6 %fusion.2 = (bf16[2,112,2560]{2,1,0:T(8,128)(2,1)}, f32[2,112,2560]{2,1,0:T(8,128)}, f32[2,112,2560]{2,1,0:T(8,128)}, bf16[2,112,2560]{2,1,0:T(8,128)(2,1)}, f32...) fusion(bf16[2,112,2560]{2,1,0:T(8,128)(2,1)S(1)} %copy-done.1, f32[]{:T(128)S(6)} %min_shard_map.3, ...), kind=kLoop, calls=%fused_computation.11 | loop fusion | flops 22937600 | bytes 25231364 | tf_op jit(solution)/shard_map/convert_element_type | solution.py:804
  (23 shorter events, 0.2 us)
Async XLA Ops:
  7.2 2.5 copy-start
  7.2 40.3 %all-gather.17.cloned.1.call-start = ((), (), s32[]{:S(2)}) async-start(), calls=%async_computation.2 | async-start | bytes 5160960 | tf_op jit(solution)/shard_map/all_gather | solution.py:814
  9.6 1.7 copy-start.2
  9.7 74.5 %all-gather.13.cloned.1.call-start = ((), (), s32[]{:S(2)}) async-start(), calls=%async_computation | async-start | bytes 5160960 | tf_op jit(solution)/shard_map/all_gather | solution.py:814
  10.8 110.0 %all-gather.15.cloned.1.call-start = ((), (), s32[]{:S(2)}) async-start(), calls=%async_computation.1 | async-start | bytes 5160960 | tf_op jit(solution)/shard_map/all_gather | solution.py:814
  12.4 191.0 %all-gather.19.cloned.1.call-start = ((), (), s32[]{:S(2)}) async-start(), calls=%async_computation.3 | async-start | bytes 5160960 | tf_op jit(solution)/shard_map/all_gather | solution.py:814
  13.0 190.4 %all-gather.21.cloned.1.call-start = ((), (), s32[]{:S(2)}) async-start(), calls=%async_computation.4 | async-start | bytes 5160960 | tf_op jit(solution)/shard_map/all_gather | solution.py:814
  13.6 216.8 %all-gather.23.cloned.1.call-start = ((), (), s32[]{:S(2)}) async-start(), calls=%async_computation.5 | async-start | bytes 5160960 | tf_op jit(solution)/shard_map/all_gather | solution.py:814
  592.6 6.6 %copy-start.1 = (bf16[2,112,2560]{2,1,0:T(8,128)(2,1)S(1)}, bf16[2,112,2560]{2,1,0:T(8,128)(2,1)}, u32[]{:S(2)}) copy-start(bf16[2,112,2560]{2,1,0:T(8,128)(2,1)} %param.13) | copy-start | bytes 3440644
  592.6 6.6 %copy-start.3 = (bf16[2,112,2560]{2,1,0:T(8,128)(2,1)S(1)}, bf16[2,112,2560]{2,1,0:T(8,128)(2,1)}, u32[]{:S(2)}) copy-start(bf16[2,112,2560]{2,1,0:T(8,128)(2,1)} %param.14) | copy-start | bytes 3440644
  592.6 6.6 %copy-start.4 = (f32[2,112,2560]{2,1,0:T(8,128)S(1)}, f32[2,112,2560]{2,1,0:T(8,128)}, u32[]{:S(2)}) copy-start(f32[2,112,2560]{2,1,0:T(8,128)} %param.19) | copy-start | bytes 6881284
  592.6 6.6 %copy-start.5 = (f32[2,112,2560]{2,1,0:T(8,128)S(1)}, f32[2,112,2560]{2,1,0:T(8,128)}, u32[]{:S(2)}) copy-start(f32[2,112,2560]{2,1,0:T(8,128)} %param.16) | copy-start | bytes 6881284
  592.7 7.7 %copy-start.6 = (f32[2,112,2560]{2,1,0:T(8,128)S(1)}, f32[2,112,2560]{2,1,0:T(8,128)}, u32[]{:S(2)}) copy-start(f32[2,112,2560]{2,1,0:T(8,128)} %param.20) | copy-start | bytes 6881284
  592.7 8.4 %copy-start.7 = (f32[2,112,2560]{2,1,0:T(8,128)S(1)}, f32[2,112,2560]{2,1,0:T(8,128)}, u32[]{:S(2)}) copy-start(f32[2,112,2560]{2,1,0:T(8,128)} %param.17) | copy-start | bytes 6881284
  592.7 8.4 %copy-start.8 = (bf16[112,2560]{1,0:T(8,128)(2,1)S(1)}, bf16[112,2560]{1,0:T(8,128)(2,1)}, u32[]{:S(2)}) copy-start(bf16[112,2560]{1,0:T(8,128)(2,1)} %get-tuple-element.25) | copy-start | bytes 1720324
  592.7 8.6 %copy-start.9 = (bf16[112,2560]{1,0:T(8,128)(2,1)S(1)}, bf16[112,2560]{1,0:T(8,128)(2,1)}, u32[]{:S(2)}) copy-start(bf16[112,2560]{1,0:T(8,128)(2,1)} %get-tuple-element.28) | copy-start | bytes 1720324
Sparse Core Ops, SparseCore 0:
  10.4 37.0 all-gather.16
  49.9 34.1 all-gather.12
  86.5 34.1 all-gather.14
  123.1 34.2 all-gather.18
  159.6 34.2 all-gather.20
  196.1 34.1 all-gather.22

commit v3 on v0

v3 whole, which is shorter than its diff:
```python
import functools
import re

import jax
import jax.numpy as jnp
from jax import lax
from jax.experimental import pallas as pl
from jax.experimental.pallas import tpu as pltpu
from jax.sharding import PartitionSpec as P

bf16, f32 = jnp.bfloat16, jnp.float32
CH, SUB, TM, LANES, ROWS, UNIT = 256, 512, 1024, 128, 256, 64
HALF, BOTH = UNIT // 2, 2 * CH
SMALL, TWO, TWO_THREE = (8, LANES), (2,), (2, 3)
PAIR = range(2)
NT_DIMS = (((1,), (1,)), ((), ()))
TN_DIMS = (((0,), (0,)), ((), ()))
VMEM_LIMIT = 67043328
MESH = pl.DeviceIdType.MESH
EPS = 1e-6
LAST_CHUNK, LAST_ROUND = 9, 4
ANY = pl.BlockSpec(memory_space=pl.ANY)
V, DMA, REGULAR = pltpu.VMEM, pltpu.SemaphoreType.DMA, pltpu.SemaphoreType.REGULAR
local = pltpu.make_async_copy


NORM_PLAN = "s0s1//s2/"
TILE_PLAN = "".join((
    "f0x0c0f1f2s3/s4/x1c1x2s5/c2f3s6/f4/",
    "x3f5s7/c3f6x4s8/c4x5s9/c5x6f7/c6f8s10/",
    "f9/x7x8/c7c8s11/x9f10/c9s12/",
    "f11/x10s13/c10f12/x11/c11s14/",
))
DOWN_PLAN = "x12c12f13//f14/x13/c13x14/c14//"
END_PLAN = ""


def odd(i):
    return i % 2


def groups_of(i):
    first = i // 2 + 10 * odd(i)
    return first * LANES, (first + 5) * LANES


def dot(a, b):
    return jnp.dot(a, b, preferred_element_type=f32)


def dot_nt(a, b):
    return lax.dot_general(a, b, NT_DIMS, preferred_element_type=f32)


def dot_tn(a, b):
    return lax.dot_general(a, b, TN_DIMS, preferred_element_type=f32)


def at(start, size, multiple=None):
    return pl.ds(pl.multiple_of(start, multiple or size), size)


def block(t, size):
    return at(t * size, size)


def wide(x):
    return x.astype(f32)


def sigmoid(x):
    return 1.0 / (1.0 + jnp.exp(-x))


def start(*copies):
    for c in copies:
        c.start()


def wait(*copies):
    for c in copies:
        c.wait()


def loop(count, body, first=0):
    def turn(t, carry):
        body(t)
        return carry

    lax.fori_loop(first, count, turn, 0)


def when(condition):
    if isinstance(condition, bool):
        return (lambda f: f()) if condition else (lambda f: None)
    return pl.when(condition)


def unless(condition):
    return when(not condition if isinstance(condition, bool) else jnp.logical_not(condition))


def branch(condition):
    if isinstance(condition, bool):
        return when(condition)
    return lambda f: loop(condition.astype(jnp.int32), lambda _: f())


def both(a, b):
    return a and b if isinstance(a, bool) and isinstance(b, bool) else jnp.logical_and(a, b)


def rows_in(w_hbm, buf, sem, i):
    return [local(w_hbm.at[at(s, LANES), :], buf.at[block(n, LANES), :], sem.at[n]) for n, s in enumerate(groups_of(i))]


def norm_scale(w):
    return lax.rsqrt(jnp.mean(w * w, -1, keepdims=True) + EPS)


def normed(w):
    return (w * norm_scale(w)).astype(bf16)


class Place:
    def __init__(self):
        self.s = s = lax.axis_index("s")
        self.c, self.y, self.x = odd(s), odd(s // 2), s // 4
        other, across_x, across_y = 1 - 2 * self.c, 4 - 8 * self.x, 2 - 4 * self.y
        self.core, self.over_x, self.over_y = {"s": s + other}, {"s": s + across_x}, {"s": s + across_y}
        self.over_z = {"r": 1 - lax.axis_index("r")}
        self.mine = (s, s + across_x, s + across_y, s + across_x + across_y)
        self.others = tuple(o + other for o in self.mine)
        self.peers = self.mine[1:] + self.others

    def barrier(self, across=True, all_peers=False):
        barrier = pltpu.get_barrier_semaphore()
        neighbours = [{"s": s} for s in self.peers] if all_peers else [self.core, self.over_y, self.over_x]
        if across:
            neighbours.append(self.over_z)
        for device in neighbours:
            give(barrier, device)
        pl.semaphore_wait(barrier, len(neighbours))


def remote(source, target, send, receive, device):
    return pltpu.make_async_remote_copy(source, target, send, receive, device_id=device, device_id_type=MESH)


def give(semaphore, device):
    pl.semaphore_signal(semaphore, inc=1, device_id=device, device_id_type=MESH)


def take(semaphore):
    pl.semaphore_wait(semaphore, 1)


class Reducer:
    SHAPES = ("ocp", "cp", "pp", "pp", "p", "p", "p", "p", "p")

    @classmethod
    def scratch(cls, shape):
        sizes = {"o": (2, 4), "c": (4,), "p": (2,)}
        buffers = [V((2,) + sum((sizes[c] for c in lead if c != "c" or "o" not in lead), ()) + shape, bf16) for lead in cls.SHAPES]
        one, two = (2,), (2, 2)
        return buffers + [DMA((2,) + n) for n in (one, two, two, one)] + [REGULAR(n) for n in (one, two, two, one)] + [V((8, shape[1]), f32)]

    COUNT = 18

    def __init__(self, place, refs):
        self.place = place
        self.all, self.got0, self.out1, self.got1, self.out2, self.got2, self.out3, self.got3, self.out = refs[:9]
        self.sem0, self.sem1, self.sem2, self.sem3, self.free0, self.free1, self.free2, self.free3, self.squares = refs[9:]
        self.squares[...] = jnp.zeros_like(self.squares)
        self.first_way, self.second_way = (place.over_x, place.over_y), (place.over_y, place.over_x)

    def copy0(self, b):
        return remote(self.all.at[b, 1 - self.place.c], self.got0.at[b], self.sem0.at[0, b], self.sem0.at[1, b], self.place.core)

    def copy1(self, b, p):
        return remote(self.out1.at[b, p], self.got1.at[b, p], self.sem1.at[0, b, p], self.sem1.at[1, b, p], self.first_way[p])

    def copy2(self, b, p):
        return remote(self.out2.at[b, p], self.got2.at[b, p], self.sem2.at[0, b, p], self.sem2.at[1, b, p], self.second_way[p])

    def copy3(self, b):
        return remote(self.out3.at[b], self.got3.at[b], self.sem3.at[0, b], self.sem3.at[1, b], self.place.over_z)

    def chip_sum(self, b, p, x, y):
        k = 2 * x + y
        return wide(self.all[b, self.place.c, k, p]) + wide(self.got0[b, k, p])

    def send(self, b, first, final):
        unless(first)(lambda: take(self.free0.at[b]))
        self.copy0(b).start()

    def after_core(self, b, first, final):
        place = self.place
        self.copy0(b).wait()
        for p in PAIR:
            unless(first)(lambda: take(self.free1.at[b, p]))
            for n in PAIR:
                self.out1[b, p, n] = self.chip_sum(b, p, *((n, 1 - place.y) if p else (1 - place.x, n))).astype(bf16)
            self.copy1(b, p).start()

    def after_first(self, b, first, final):
        place = self.place
        for p in PAIR:
            self.copy1(b, p).wait()
            unless(first)(lambda: take(self.free2.at[b, p]))
            away = (1 - place.x, place.y) if p else (place.x, 1 - place.y)
            self.out2[b, p] = (self.chip_sum(b, p, *away) + wide(self.got1[b, p, away[1 - p]])).astype(bf16)
            self.copy2(b, p).start()

    def after_second(self, b, first, final):
        place = self.place
        for p in PAIR:
            self.copy2(b, p).wait()
            near = place.x if p else place.y
            self.out3[b, p] = (self.chip_sum(b, p, place.x, place.y) + wide(self.got1[b, p, near]) + wide(self.got2[b, p])).astype(bf16)
        unless(first)(lambda: take(self.free3.at[b]))
        self.copy3(b).start()

        def release():
            give(self.free0.at[b], place.core)
            for p in PAIR:
                give(self.free1.at[b, p], self.first_way[p])
                give(self.free2.at[b, p], self.second_way[p])

        unless(final)(release)

    def after_copy(self, b, first, final):
        self.copy3(b).wait()
        for p in PAIR:
            g = (wide(self.out3[b, p]) + wide(self.got3[b, p])).astype(bf16)
            self.out[b, p] = g
            g = wide(g)
            self.squares[...] += jnp.sum((g * g).reshape(-1, 8, g.shape[1]), 0)
        unless(final)(lambda: give(self.free3.at[b], self.place.over_z))


class Steps:
    def __init__(self, weights, layer, land, me, span=1, stage=None, first=0):
        self.weights, self.layer, self.land, self.me, self.span, self.stage, self.first = weights, layer, land, me, span, stage, first

    def own(self, q):
        return self.region(q, self.me) if self.stage is None else self.staged(q)


class WideSteps(Steps):
    @property
    def rows(self):
        return self.weights[0].shape[1]

    def region(self, q, owner):
        return self.land.at[pl.ds(q, self.span), at(self.rows * owner, self.rows, 16), :]

    def part(self, q, owner, p):
        return self.land.at[pl.ds(q, self.span), at(self.rows * owner, self.rows, 16), block(p, CH)]

    def staged(self, q):
        return self.stage.at[pl.ds(q - self.first, self.span)]

    def fetch(self, q, sem):
        for k in range(self.span):
            for p in PAIR:
                for n, s in enumerate(groups_of(q + k)):
                    lanes = at(CH * p + LANES * n, LANES)
                    if self.stage is None:
                        target = self.land.at[q + k, at(self.rows * self.me, self.rows, 16), lanes]
                    else:
                        target = self.stage.at[q + k - self.first, :, lanes]
                    local(self.weights[p].at[self.layer, :, at(s, LANES)], target, sem).start()


class DownSteps(Steps):
    @property
    def rows(self):
        return self.weights.shape[1]

    def region(self, q, owner):
        return self.land.at[at(self.rows * owner + UNIT * q, UNIT * self.span, UNIT), :]

    def part(self, q, owner, p):
        return self.land.at[at(self.rows * owner + UNIT * q + HALF * self.span * p, HALF * self.span, HALF), :]

    def staged(self, q):
        return self.stage.at[at(UNIT * (q - self.first), UNIT * self.span, UNIT), :]

    def fetch(self, q, sem):
        local(self.weights.at[self.layer, at(UNIT * q, UNIT * self.span, UNIT), :], self.own(q), sem).start()


class Gatherer:
    @staticmethod
    def scratch(steps):
        return [DMA((steps, 8)), DMA((2, 8)), DMA((steps,)), DMA((steps,))]

    COUNT = 4

    def __init__(self, place, steps, refs):
        self.place, self.steps = place, steps
        self.received, self.sent, self.fetched, self.homed = refs

    def each(self, m, f):
        for k, (kind, q) in enumerate(self.steps):
            branch(m == k)(functools.partial(f, kind, q, k))

    def copy(self, m, n, source, target, device):
        return remote(source, target, self.sent.at[odd(m), n], self.received.at[m, n], device)

    def push(self, m, n, region, device, source=None):
        copy = self.copy(m, n, region if source is None else source, region, device)
        if m >= 2:
            self.gone(m - 2, n)
        copy.start()

    def gone(self, m, n):
        kind, q = self.steps[m]
        region = kind.part(q, self.place.s, 0) if n in (4, 6) else kind.region(q, self.place.s)
        self.copy(m, n, region, region, self.place.core).wait_send()

    def landed(self, m, n, target):
        self.copy(m, n, target, target, self.place.core).wait_recv()

    def home(self, kind, q, m):
        return local(kind.own(q), kind.region(q, kind.me), self.homed.at[m])

    def fetch_all(self):
        for m, (kind, q) in enumerate(self.steps):
            kind.fetch(q, self.fetched.at[m])

    def spread(self, m):
        def act(kind, q, m):
            own, target = kind.own(q), kind.region(q, kind.me)
            local(own, own, self.fetched.at[m]).wait()
            for n, device in ((1, self.place.over_x), (2, self.place.over_y), (0, self.place.core)):
                self.push(m, n, target, device, own)
            if kind.stage is not None:
                self.home(kind, q, m).start()

        self.each(m, act)

    def forward(self, m):
        def act(kind, q, m):
            for p, device in enumerate((self.place.over_y, self.place.over_x)):
                owner = self.place.mine[1 + p]
                region, part = kind.region(q, owner), kind.part(q, owner, p)
                self.landed(m, 1 + p, region)
                self.push(m, 4 + 2 * p, part, device)
                self.push(m, 3 + 2 * p, region, self.place.core)

        self.each(m, act)

    def cross(self, m):
        def act(kind, q, m):
            for p in PAIR:
                self.landed(m, 4 + 2 * p, kind.part(q, self.place.mine[3], p))
            self.push(m, 7, kind.region(q, self.place.mine[3]), self.place.core)

        self.each(m, act)

    def complete(self, m):
        def act(kind, q, m):
            for n, owner in zip((0, 3, 5, 7), self.place.others):
                self.landed(m, n, kind.region(q, owner))
            if kind.stage is not None:
                self.home(kind, q, m).wait()

        self.each(m, act)

    def finish(self):
        for m in range(len(self.steps) - 2, len(self.steps)):
            for n in range(8):
                self.gone(m, n)


class Gradients:
    @staticmethod
    def scratch(rows, D, rounds):
        return Reducer.scratch((rows, CH)) + Reducer.scratch((HALF, D)) + [V((rounds, UNIT, D), bf16), DMA((2, 2, 2)), DMA((rounds,)), DMA(TWO_THREE)]

    def __init__(self, place, refs, outs, pieces, rounds, early=None):
        n = Reducer.COUNT
        self.place, self.pieces, self.rounds = place, pieces, rounds
        self.wide = Reducer(place, refs[:n])
        self.down = Reducer(place, refs[n : n + n])
        self.down_out, self.out_sem, self.local_sem, self.cross_sem = refs[n + n :]
        self.outs, self.early = outs, early
        self.before = 0 if early is None else 1

    def put_wide(self, p, value):
        b, rows = odd(p), value.shape[0] // 8
        value = value.astype(bf16)
        for s in range(8):
            for part in PAIR:
                self.wide.all[b, odd(s), s // 2, part] = value[rows * s : rows * (s + 1), CH * part : CH * (part + 1)]

    def put_down(self, i, q, value):
        value = value.astype(bf16)
        for n in PAIR:
            for core in PAIR:
                for part in PAIR:
                    row = LANES * n + UNIT * core + HALF * part
                    self.down.all[odd(q), core, 2 * odd(i) + n, part] = value[row : row + HALF]

    def flags(self, p):
        return odd(p), p < 2, p + 2 >= self.pieces

    def wide_send(self, p):
        self.wide.send(*self.flags(p))

    def wide1(self, p):
        self.wide.after_core(*self.flags(p))

    def wide2(self, p):
        self.wide.after_first(*self.flags(p))

    def wide3(self, p):
        self.wide.after_second(*self.flags(p))

    def wide_outs(self, b, i, outs):
        return [
            local(self.wide.out.at[b, part, :, block(n, LANES)], outs[part].at[:, at(s, LANES)], self.out_sem.at[b, part, n])
            for part in PAIR
            for n, s in enumerate(groups_of(i))
        ]

    def wide_gone(self, p):
        wait(*self.wide_outs(odd(p), 0, self.outs))

    def wide4(self, p):
        unless(p < 2)(lambda: self.wide_gone(p - 2))
        self.wide.after_copy(*self.flags(p))
        if self.before:
            when(p == 0)(lambda: start(*self.wide_outs(0, LAST_CHUNK, self.early)))
        when(p >= self.before)(lambda: start(*self.wide_outs(odd(p), p - self.before, self.outs)))

    def round_flags(self, q):
        return odd(q), q < 2, q + 2 >= self.rounds

    def down_send(self, q):
        self.down.send(*self.round_flags(q))

    def down1(self, q):
        self.down.after_core(*self.round_flags(q))

    def down2(self, q):
        self.down.after_first(*self.round_flags(q))

    def down3(self, q):
        self.down.after_second(*self.round_flags(q))

    def down_copies(self, q, j, outs, n):
        unit = 2 * j + self.place.c
        target = outs[2].at[block(unit % 5, UNIT), :]
        cross = remote(self.down_out.at[q], target, self.cross_sem.at[0, n], self.cross_sem.at[1, n], self.place.core)
        return unit // 5 == self.place.c, local(self.down_out.at[q], target, self.local_sem.at[q]), cross

    def down_start(self, q, j, outs, n):
        mine, here, cross = self.down_copies(q, j, outs, n)
        when(mine)(here.start)
        unless(mine)(cross.start)

    def down4(self, q):
        self.down.after_copy(*self.round_flags(q))
        for part in PAIR:
            self.down_out[q, block(part, HALF), :] = self.down.out[odd(q), part]
        j = q - self.before
        if self.before:
            when(q == 0)(lambda: self.down_start(q, LAST_ROUND, self.early, 2))
        when(j >= 0)(lambda: self.down_start(q, j, self.outs, j % 3))

    def squares(self):
        refs = (self.wide.squares, self.down.squares)
        return sum(ref[:, block(n, LANES)] for ref in refs for n in range(ref.shape[1] // LANES))

    def finish(self):
        for p in (self.pieces - 2, self.pieces - 1):
            self.wide_gone(p)
        for q in range(self.rounds):
            j, outs = q - self.before, self.outs
            n = j % 3
            if j < 0:
                j, outs, n = LAST_ROUND, self.early, 2
            mine, here, cross = self.down_copies(q, j, outs, n)
            when(mine)(here.wait)
            unless(mine)(cross.wait_send)
            theirs = (2 * j + 1 - self.place.c) // 5
            when(theirs == self.place.c)(cross.wait_recv)


def forward_kernel(h_hbm, wg_hbm, wu_hbm, wd_hbm, kept_hbm, out_hbm, a_hbm, aT_hbm, turned_hbm, down_hbm, next_wide_hbm, next_down_hbm,
                   a_ref, act_ref, wgu, wd, wide_stage, down_stage, gus, turn, hin, hout, aout, aTout, hsem, gsem, tsem, xsem, osem, dsem, *refs):
    T, D = a_ref.shape
    F = act_ref.shape[1]
    TILE = gus.shape[1]
    NC, NT, parts = F // CH, T // TILE, TILE // SUB
    place = Place()
    pair = (wg_hbm, wu_hbm)
    ones, downs, last_down = WideSteps(pair, 0, wgu, place.s), DownSteps(wd_hbm, 0, wd, place.s, 2), DownSteps(wd_hbm, 0, wd, place.s)
    gatherer = Gatherer(
        place,
        tuple((ones, i) for i in range(NC))
        + ((downs, 0), (downs, 2), (last_down, 4))
        + ((DownSteps(wd_hbm, 1, next_down_hbm, place.s, 2, down_stage), 0), (WideSteps(pair, 1, next_wide_hbm, place.s, 2, wide_stage), 0)),
        refs,
    )
    spread, forward, cross, complete = gatherer.spread, gatherer.forward, gatherer.cross, gatherer.complete

    def gather(plan):
        for name, m in re.findall("([sfxc])([0-9]+)", plan):
            {"s": spread, "f": forward, "x": cross, "c": complete}[name](int(m))

    def follow(plans, t, few=5):
        plans = plans.split("/")

        def one_of(first):
            for k, plan in enumerate(plans[first : first + few]):
                if plan:
                    branch(t == first + k)(lambda: gather(plan))

        for first in range(0, len(plans), few):
            branch(both(t >= first, t < first + few))(lambda: one_of(first))

    def load(t):
        rows = block(t, ROWS)
        return local(h_hbm.at[rows, :], a_ref.at[rows, :], hsem.at[t])

    def save(n):
        return local(gus.at[odd(n)], kept_hbm.at[n // NT, block(n % NT, TILE), :], gsem.at[odd(n)])

    def turned(t):
        return local(turn.at[odd(t)], turned_hbm.at[:, block(t, ROWS)], tsem.at[odd(t)])

    gatherer.fetch_all()
    loop(T // ROWS, lambda t: load(t).start())
    place.barrier(across=False)
    def norm(t):
        load(t).wait()
        rows = block(t, ROWS)
        a = normed(wide(a_ref[rows, :]))
        a_ref[rows, :] = a
        unless(t < 2)(lambda: turned(t - 2).wait())
        turn[odd(t)] = a.T
        turned(t).start()

    for k, plan in enumerate(NORM_PLAN.split("/")):
        gather(plan)
        loop(4 * k + 4, norm, 4 * k)

    def tile(n):
        i, t, b = n // NT, n % NT, odd(n)
        follow(TILE_PLAN, n)
        unless(n < 2)(lambda: save(n - 2).wait())

        def dots(k):
            gu = dot(a_ref[block(parts * t + k, SUB), :], wgu[i])
            gus[b, block(k, SUB), :] = gu
            return gu

        def elementwise(k, gu):
            gate, up = gu[:, :CH], gu[:, CH:]
            act = (gate * sigmoid(gate) * up).astype(bf16)
            for run, s in enumerate(groups_of(i)):
                act_ref[block(parts * t + k, SUB), at(s, LANES)] = act[:, LANES * run : LANES * (run + 1)]

        gu = dots(0)
        for k in range(parts):
            following = dots(k + 1) if k + 1 < parts else None
            elementwise(k, gu)
            gu = following
        save(n).start()

    loop(NC * NT, tile)
    gather(DOWN_PLAN.split("/")[0])
    down_out = local(wd, down_hbm, dsem)
    down_out.start()

    def inputs(t):
        return local(h_hbm.at[block(t, SUB), :], hin.at[odd(t)], xsem.at[odd(t)])

    def outputs(t):
        b, rows = odd(t), block(t, SUB)
        return local(hout.at[b], out_hbm.at[rows, :], osem.at[b, 0])

    def norms(t):
        b, rows = odd(t), block(t, SUB)
        return local(aout.at[b], a_hbm.at[rows, :], osem.at[b, 1]), local(aTout.at[b], aT_hbm.at[:, rows], osem.at[b, 2])

    count = T // SUB

    def norm_next(t):
        b = odd(t)
        a = normed(wide(hout[b]))
        aout[b] = a
        aTout[b] = a.T
        start(*norms(t))

    def down(t):
        branch(t > 0)(lambda: follow(DOWN_PLAN, t))
        b = odd(t)
        inputs(t).wait()
        when(t + 1 < count)(lambda: inputs(t + 1).start())
        unless(t < 2)(lambda: outputs(t - 2).wait())
        unless(t < 3)(lambda: wait(*norms(t - 3)))
        before = normed(wide(hout[1 - b]))
        aout[1 - b] = before
        aTout[1 - b] = before.T
        out = dot(act_ref[block(t, SUB), :], wd[...]).astype(bf16)
        hout[b] = (wide(hin[b]) + wide(out)).astype(bf16)
        outputs(t).start()
        unless(t < 1)(lambda: start(*norms(t - 1)))

    inputs(0).start()
    hout[1] = jnp.zeros_like(hout[1])
    loop(count, down)
    wait(*norms(count - 3))
    norm_next(count - 1)
    gather(END_PLAN)
    for n in (NC * NT - 2, NC * NT - 1):
        save(n).wait()
    for t in PAIR:
        turned(T // ROWS - 2 + t).wait()
        wait(outputs(count - 2 + t), *norms(count - 2 + t))
    down_out.wait()
    gatherer.finish()


def silu_back(dact, gate, up, act_ref, dgu_ref, rows):
    dact = wide(dact.astype(bf16))
    sg = sigmoid(gate)
    silu = gate * sg
    act_ref[rows, :] = (silu * up).astype(bf16)
    dgate = (dact * up * (sg + silu * (1.0 - sg))).astype(bf16)
    dup = (dact * silu).astype(bf16)
    dgu_ref[rows, block(0, CH)] = dgate
    dgu_ref[rows, block(1, CH)] = dup
    return dgate, dup


def middle_kernel(h_hbm, a_hbm, aT_hbm, dy_hbm, wg_hbm, wu_hbm, wd_hbm, wide_in, down_in, gg_hbm, gu_hbm, gd_hbm, dh_hbm, sq_hbm, wide_left, down_left, wide_hbm, down_hbm,
                  a_ref, aT_ref, dy_ref, da_ref, dgu_ref, act_ref, wgu, wd, sq, wide_stage, down_stage, hsem, asem, ysem, tsem, wsem, qsem, left_sem, *refs):
    T, D = a_ref.shape
    F = wg_hbm.shape[2]
    NC, NT = F // CH, T // TM
    n_blocks = T // ROWS

    def load(t):
        rows = block(t, ROWS)
        return local(h_hbm.at[rows, :], a_ref.at[rows, :], hsem.at[t])

    def states(t):
        rows = block(t, TM)
        return local(a_hbm.at[rows, :], a_ref.at[rows, :], asem.at[t]), local(dy_hbm.at[rows, :], dy_ref.at[rows, :], ysem.at[t])

    turned = local(aT_hbm, aT_ref, tsem)

    def weights(i):
        b = odd(i)
        return [local(wide_hbm.at[i], wgu.at[b], wsem.at[b, 2])] + rows_in(down_hbm, wd.at[b], wsem.at[b], i)

    start(*states(0))
    start(*weights(0))
    for t in range(1, NT):
        start(*states(t))
    turned.start()
    place = Place()
    gradients = Gradients(place, refs[Gatherer.COUNT :], (gg_hbm, gu_hbm, gd_hbm), NC - 1, NC // 2 - 1)
    wides = WideSteps((wg_hbm, wu_hbm), 1, wide_hbm, place.s, 2, wide_stage, 2)
    downs, last_down = (DownSteps(wd_hbm, 1, down_hbm, place.s, span, down_stage, 2) for span in (2, 1))
    gatherer = Gatherer(place, ((downs, 2), (wides, 2), (last_down, 4), (wides, 4), (wides, 6), (wides, 8)), refs[: Gatherer.COUNT])
    gatherer.fetch_all()
    place.barrier()
    gatherer.spread(0)

    def clear(t):
        da_ref[block(t, ROWS), :] = jnp.zeros((ROWS, D), f32)

    loop(n_blocks, clear)

    def gather_start():
        gatherer.forward(0)
        gatherer.spread(1)

    def gather_first(i):
        branch(i >= 1)(lambda: gatherer.cross(i))
        branch(i >= 1)(lambda: gatherer.spread(i + 1))

    def gather_last(i):
        branch(i == 0)(lambda: gatherer.cross(0))
        branch(i >= 1)(lambda: gatherer.forward(i + 1))
        branch(i >= 1)(lambda: gatherer.complete(i))

    def gather_between(i):
        branch(i == 0)(lambda: gatherer.complete(0))
        branch(i == 0)(lambda: gatherer.forward(1))

    def in_tiles(i):
        branch(i >= 1)(lambda: gradients.wide1(i - 1))
        branch(i >= 3)(lambda: gradients.wide4(i - 3))

    wide_over = local(gradients.wide.all.at[odd(NC - 1)], wide_left, left_sem.at[0])
    down_over = local(gradients.down.all.at[odd(NC // 2 - 1)], down_left, left_sem.at[1])

    def after_down(i):
        j = i // 2

        def odd_one():
            branch(i >= 3)(lambda: gradients.down4(j - 1))
            branch(i < NC - 1)(lambda: gradients.down_send(j))
            when(i == NC - 1)(down_over.start)

        branch(odd(i) == 1)(odd_one)
        branch(both(odd(i) == 0, i >= 2))(lambda: gradients.down2(j - 1))
        branch(i >= 2)(lambda: gradients.wide3(i - 2))

    def after_wide(i):
        j = i // 2
        branch(i < NC - 1)(lambda: gradients.wide_send(i))
        when(i == NC - 1)(wide_over.start)
        branch(i >= 1)(lambda: gradients.wide2(i - 1))
        branch(both(odd(i) == 1, i < NC - 1))(lambda: gradients.down1(j))
        branch(both(odd(i) == 0, i >= 2))(lambda: gradients.down3(j - 1))

    def chunk(i):
        b = odd(i)
        wait(*weights(i))

        def tile(t):
            when(i == 0)(lambda: wait(*states(t)))
            branch(t == 0)(lambda: gather_first(i))
            branch(both(t == 1, i == 0))(lambda: gather_start())
            branch(t == 2)(lambda: in_tiles(i))
            branch(t == 3)(lambda: gather_last(i))

            def dots(k):
                rows = block(2 * t + k, SUB)
                return dot(a_ref[rows, :], wgu[b]), dot_nt(dy_ref[rows, :], wd[b])

            def elementwise(k, gu, dact):
                return jnp.concatenate(silu_back(dact, gu[:, :CH], gu[:, CH:], act_ref, dgu_ref, block(2 * t + k, SUB)), 1)

            def back(k, dgu):
                da_ref[block(2 * t + k, SUB), :] += dot_nt(dgu, wgu[b])

            now = dots(0)
            following = dots(1)
            dgu = elementwise(0, *now)
            dgu_next = elementwise(1, *following)
            back(0, dgu)
            back(1, dgu_next)

        loop(NT, tile)
        gradients.put_down(i, i // 2, dot_tn(act_ref[...], dy_ref[...]))
        after_down(i)
        gather_between(i)
        when(i + 1 < NC)(lambda: start(*weights(i + 1)))
        when(i == 0)(turned.wait)
        gradients.put_wide(i, dot(aT_ref[...], dgu_ref[...]))
        after_wide(i)

    loop(NC, chunk)
    loop(n_blocks, lambda t: load(t).start())

    def store(t):
        rows = block(t, ROWS)
        return local(dy_ref.at[rows, :], dh_hbm.at[rows, :], hsem.at[t])

    def norm_back(t):
        rows = block(t, ROWS)
        load(t).wait()
        w = wide(a_ref[rows, :])
        da = wide(da_ref[rows, :].astype(bf16))
        scale = norm_scale(w)
        along = jnp.sum(da * w, -1, keepdims=True) * (scale * scale * scale) * (1.0 / D)
        by_h = (da * scale - w * along).astype(bf16)
        dy_ref[rows, :] = (wide(dy_ref[rows, :]) + wide(by_h)).astype(bf16)
        store(t).start()
        branch(t == n_blocks // 2)(lambda: gradients.wide3(NC - 2))

    gradients.wide4(NC - 3)
    loop(n_blocks, norm_back)
    gradients.wide4(NC - 2)
    sq[...] = gradients.squares()
    done = local(sq, sq_hbm, qsem)
    done.start()
    loop(n_blocks, lambda t: store(t).wait())
    gradients.finish()
    gatherer.finish()
    wait(wide_over, down_over)
    done.wait()


def last_kernel(aT_hbm, dy_hbm, kept_hbm, wd_hbm, sq_in, wide_left, down_left, eg_in, eu_in, ed_in, gg_hbm, gu_hbm, gd_hbm, sq_hbm, eg_hbm, eu_hbm, ed_hbm,
                aT_ref, dy_ref, even_dgu, even_act, odd_dgu, odd_act, by_gu, by_d, gus, wd, sq, parts, ysem, tsem, gsem, wsem, qsem, psem, left_sem, *refs):
    D, T = aT_ref.shape
    F = wd_hbm.shape[0]
    NC, NT = F // CH, T // TM
    depth = gus.shape[0]

    def states(t):
        rows = block(t, TM)
        return local(dy_hbm.at[rows, :], dy_ref.at[rows, :], ysem.at[t])

    def turned(t):
        rows = block(t, TM)
        return local(aT_hbm.at[:, rows], aT_ref.at[:, rows], tsem.at[t])

    def weights(i):
        b = odd(i)
        return rows_in(wd_hbm, wd.at[b], wsem.at[b], i)

    def kept(n):
        return local(kept_hbm.at[n // NT, block(n % NT, TM), :], gus.at[n % depth], gsem.at[n % depth])

    start(*weights(0))
    for t in range(NT):
        start(states(t), turned(t))
        if t < depth:
            kept(t).start()
    before = local(sq_in, sq, qsem)
    before.start()
    place = Place()
    gradients = Gradients(place, refs, (gg_hbm, gu_hbm, gd_hbm), NC + 1, NC // 2 + 1, (eg_hbm, eu_hbm, ed_hbm))
    left = [local(x, r.all.at[0], left_sem.at[n]) for n, (x, r) in enumerate(((wide_left, gradients.wide), (down_left, gradients.down)))]
    start(*left)
    place.barrier(all_peers=True)

    def add(ref, term, fresh):
        ref[...] = (ref[...] if fresh is None else jnp.where(fresh, 0.0, ref[...])) + term

    def terms_gu(t, dgu_ref, fresh=None):
        add(by_gu, dot(aT_ref[:, block(t, TM)], dgu_ref[...]), fresh)

    def terms_d(t, act_ref, fresh=None):
        add(by_d, dot_tn(act_ref[...], dy_ref[block(t, TM), :]), fresh)

    def ended(i):
        q = i // 2 + 1
        gradients.put_down(i, q, by_d[...])
        gradients.put_wide(i + 1, by_gu[...])
        gradients.wide_send(i + 1)
        branch(odd(i) == 1)(lambda: gradients.down_send(q))

    def step(n, now, before):
        some = before is not None
        i, t = n // NT, n % NT
        q = i // 2
        when(n < NT)(lambda: states(t).wait())
        if some:
            when(n <= NT)(lambda: turned(n - 1).wait())

        def next_weights():
            wait(*weights(i))
            when(i + 1 < NC)(lambda: start(*weights(i + 1)))

        when(t == 0)(next_weights)
        kept(n).wait()
        last = (t + NT - 1) % NT
        fresh = last == 0 if before is evens else None

        def dots(k):
            return dot_nt(dy_ref[block(2 * t + k, SUB), :], wd[odd(i)])

        def elementwise(k, dact):
            rows = block(k, SUB)
            silu_back(dact, gus[n % depth, rows, block(0, CH)], gus[n % depth, rows, block(1, CH)], now[1], now[0], rows)

        dact = dots(0)
        if some:
            terms_d(last, before[1], fresh)
        following = dots(1)
        elementwise(0, dact)
        if some:
            terms_gu(last, before[0], fresh)
        elementwise(1, following)
        when(n + depth < NC * NT)(lambda: kept(n + depth).start())

        def first_point():
            branch(both(odd(i) == 0, i >= 2))(lambda: gradients.down4(q - 1))
            branch(i >= 1)(lambda: ended(i - 1))
            branch(odd(i) == 1)(lambda: gradients.down2(q))

        def second_point():
            gradients.wide1(i)
            branch(i >= 1)(lambda: gradients.wide3(i - 1))

        def third_point():
            branch(odd(i) == 0)(lambda: gradients.down1(q))
            branch(odd(i) == 1)(lambda: gradients.down3(q))

        def fourth_point():
            gradients.wide2(i)
            branch(i >= 1)(lambda: gradients.wide4(i - 1))

        if some:
            for turn_at, act in enumerate((first_point, second_point, third_point, fourth_point)):
                branch(t == turn_at)(act)

    evens, odds = (even_dgu, even_act), (odd_dgu, odd_act)

    def two_steps(p):
        step(2 * p + 1, odds, evens)
        step(2 * p + 2, evens, odds)

    wait(*left)
    gradients.wide_send(0)
    gradients.down_send(0)
    step(0, evens, None)
    loop(NC * NT // 2 - 1, two_steps)
    step(NC * NT - 1 + place.s * 0, odds, evens)
    end, q = NC, NC // 2
    terms_d(NT - 1, odd_act)
    terms_gu(NT - 1, odd_dgu)
    gradients.down4(q - 1)
    ended(NC - 1)
    gradients.wide3(end - 1)
    before.wait()
    gradients.wide1(end)
    gradients.down1(q)
    gradients.wide4(end - 1)
    gradients.wide2(end)
    gradients.down2(q)
    gradients.wide3(end)
    gradients.down3(q)
    gradients.wide4(end)
    gradients.down4(q)
    sq[...] += gradients.squares()
    exchanges = [remote(sq, parts.at[n], psem.at[0, n], psem.at[1, n], {"s": s}) for n, s in enumerate(place.peers)]
    start(*exchanges)
    wait(*exchanges)
    sq[...] += sum(parts[n] for n in range(len(exchanges)))
    done = local(sq, sq_hbm, qsem)
    done.start()
    gradients.finish()
    done.wait()


def call(kernel, number, outs, scratch, inputs, aliases=None):
    return pl.pallas_call(
        kernel,
        out_shape=[jax.ShapeDtypeStruct(*o) for o in outs],
        in_specs=[ANY] * len(inputs),
        out_specs=[ANY] * len(outs),
        scratch_shapes=scratch,
        input_output_aliases=aliases or {},
        compiler_params=pltpu.CompilerParams(vmem_limit_bytes=VMEM_LIMIT, has_side_effects=True, collective_id=number),
    )(*inputs)


def forward(h, wg, wu, wd):
    (T, D), F = h.shape, wg.shape[2]
    chunks, down, states, turned = ((F // CH, D, BOTH), bf16), ((F, D), bf16), ((T, D), bf16), ((D, T), bf16)
    return call(
        forward_kernel,
        1,
        [((F // CH, T, BOTH), f32), states, states, turned, turned, down, chunks, down],
        [V(*states), V((T, F), bf16), V(*chunks), V(*down), V((2, D // 8, BOTH), bf16), V((2 * UNIT, D), bf16)]
        + [V((2, 2 * TM, BOTH), f32), V((2, D, ROWS), bf16), *[V(TWO + size, bf16) for size in [(SUB, D)] * 3 + [(D, SUB)]]]
        + [DMA((T // ROWS,)), DMA(TWO), DMA(TWO), DMA(TWO), DMA(TWO_THREE), DMA(())]
        + Gatherer.scratch(15),
        (h, wg, wu, wd),
    )


def middle(h, a, aT, dy, wg, wu, wd, chunks, down):
    (T, D), F = h.shape, wg.shape[2]
    mine, states = ((D // 8, F), bf16), ((T, D), bf16)
    return call(
        middle_kernel,
        2,
        [mine, mine, ((F // 8, D), bf16), states, (SMALL, f32)]
        + [((2, 4, 2) + size, bf16) for size in ((D // 8, CH), (HALF, D))]
        + [(chunks.shape, bf16), (down.shape, bf16)],
        [V(*states), V((D, T), bf16), V(*states), V((T, D), f32), V((T, BOTH), bf16), V((T, CH), bf16)]
        + [V((2, D, BOTH), bf16), V((2, CH, D), bf16), V(SMALL, f32), V((8, D // 8, BOTH), bf16), V((3 * UNIT, D), bf16)]
        + [DMA((T // ROWS,)), DMA((T // TM,)), DMA((T // TM,)), DMA(()), DMA(TWO_THREE), DMA(()), DMA(TWO)]
        + Gatherer.scratch(6)
        + Gradients.scratch(D // 8, D, F // CH // 2 - 1),
        (h, a, aT, dy, wg, wu, wd, chunks, down),
        {7: 7, 8: 8},
    )


def last(aT, dy, kept, wd, squares, wide_left, down_left, early):
    (D, T), F = aT.shape, wd.shape[0]
    mine = ((D // 8, F), bf16)
    return call(
        last_kernel,
        3,
        [mine, mine, ((F // 8, D), bf16), (SMALL, f32)] + [(g.shape, bf16) for g in early],
        [V((D, T), bf16), V((T, D), bf16), V((TM, BOTH), bf16), V((TM, CH), bf16), V((TM, BOTH), bf16), V((TM, CH), bf16), V((D, BOTH), f32), V((CH, D), f32)]
        + [V((3, TM, BOTH), f32), V((2, CH, D), bf16), V(SMALL, f32), V((7,) + SMALL, f32)]
        + [DMA((T // TM,)), DMA((T // TM,)), DMA((3,)), DMA((2, 2)), DMA(()), DMA((2, 7)), DMA(TWO)]
        + Gradients.scratch(D // 8, D, F // CH // 2 + 1),
        (aT, dy, kept, wd, squares, wide_left, down_left, *early),
        dict(zip(range(7, 10), range(4, 7))),
    )


def adamw(w, m, v, g):
    m = 0.9 * m + 0.1 * g
    v = 0.95 * v + 0.05 * g * g
    step = m * lax.rsqrt(v + 1e-8) + 0.1 * w
    return (w - 0.02 * step).astype(bf16), m, v


def update_kernel(count, sq_hbm, *refs):
    sources, targets, buffers, (sq, in_sem, out_sem, sq_sem) = refs[:15], refs[15:24], refs[24:36], refs[36:]
    units = [(layer, k) for layer in PAIR for k in range(3)]

    def buffer(which, layer, k):
        return buffers[3 * which + k].at[layer]

    def loads(layer, k):
        hbm = [sources[6 + 3 * which + k].at[layer] for which in range(3)] + [sources[3 * layer + k]]
        return [local(source, buffer(which, layer, k), in_sem.at[which, layer, k]) for which, source in enumerate(hbm)]

    def stores(layer, k):
        return [local(buffer(which, layer, k), targets[3 * which + k].at[layer], out_sem.at[which, layer, k]) for which in range(3)]

    size = local(sq_hbm, sq, sq_sem)
    size.start()
    for unit in units:
        start(*loads(*unit))
    size.wait()
    factor = jnp.minimum(1.0, 0.5 * lax.rsqrt(jnp.full((1, 1), jnp.sum(sq[...]) / count + 1e-30, f32)))
    for unit in units:
        wait(*loads(*unit))
        w, m, v, g = (buffer(which, *unit) for which in range(4))

        def take_step(t):
            rows = block(t, 16)
            w[rows, :], m[rows, :], v[rows, :] = adamw(wide(w[rows, :]), m[rows, :], v[rows, :], wide(g[rows, :]) * factor)

        loop(w.shape[0] // 16, take_step)
        start(*stores(*unit))
    for unit in units:
        wait(*stores(*unit))


def update(squares, count, firsts, seconds, weights, m, v):
    shapes = [jax.ShapeDtypeStruct(w.shape, kind) for kind in (bf16, f32, f32) for w in weights]
    return pl.pallas_call(
        functools.partial(update_kernel, count),
        out_shape=shapes,
        in_specs=[ANY] * 16,
        out_specs=[ANY] * len(shapes),
        scratch_shapes=[V(x.shape, x.dtype) for x in shapes + shapes[:3]] + [V(SMALL, f32), DMA((4, 2, 3)), DMA((3, 2, 3)), DMA(())],
        compiler_params=pltpu.CompilerParams(vmem_limit_bytes=VMEM_LIMIT),
    )(squares, *firsts, *seconds, *weights, *m, *v)


def solution(mesh):
    def step(x, dy, *arrays):
        weights, m, v = (arrays[i : i + 3] for i in (0, 3, 6))
        kept, h, a1, a1T, a0T, down0, chunks1, down1 = forward(x[0], *weights)
        *early, by_h, squares, wide_left, down_left, _, _ = middle(h, a1, a1T, dy[0], *weights, chunks1, down1)
        *first_sums, squares, gate1, up1, down_1 = last(a0T, by_h, kept, down0, squares, wide_left, down_left, early)
        count = lax.psum(1, "s") * sum(w.size for w in weights)
        return tuple(update(squares, count, first_sums, (gate1, up1, down_1), weights, m, v))

    states, cut = P(("rep", "r", "s"), None, None), P(None, "s", None)
    return jax.shard_map(
        step,
        mesh=mesh,
        in_specs=(states, states) + (cut,) * 9,
        out_specs=(P("rep", "s", None),) * 9,
        check_vma=False,
    )
```

time: 832 us -> 463 us (0.56)
  matrix products: 511 us -> 0 us
  Pallas kernels: 0 us -> 462 us
  waiting for transfers between devices: 216 us -> 0 us
  local copies, waits for them, and re-layouts: 33.7 us -> 0 us
  other arithmetic: 33.6 us -> 0 us
  between operations: 17 us -> 0.85 us
  blocking collectives: 13.8 us -> 0 us
    dot_general x15 -> x0, matrix products: 511 us -> none  [the longest x5 186 us: layer(): up = jnp.dot(a, w['w_up'], preferred_element_type=jnp.float32)]
    pallas_call x0 -> x4, Pallas kernels: none -> 462 us  [the longest x3 448 us: call(): pl.pallas_call(kernel, out_shape=[jax.ShapeDtypeStruct(*o) for o in outs]...]
    reduce_scatter x6 -> x0, waiting for transfers between devices: 99.5 us -> none  [summed(): lax.psum_scatter(term, 's', scatter_dimension=0, tiled=True)]
    psum x1 -> x0, waiting for transfers between devices: 91 us -> none  [summed(): lax.psum(lax.psum_scatter(term, 's', scatter_dimension=0, tiled=True), 'r')]
    unnamed x40 -> x0, local copies, waits for them, and re-layouts: 26.8 us -> none
    all_gather x6 -> x0, waiting for transfers between devices: 23.4 us -> none  [fetched(): lax.all_gather(w[number], 's', axis=0, tiled=True)]
    psum x1 -> x0, blocking collectives: 13.8 us -> none  [step(): squares = lax.psum(sum((jnp.sum(g * g) for g in gradients)), 's')]
    reduce_sum x4 -> x0, other arithmetic: 12 us -> none  [the longest x3 7.43 us: step(): squares = lax.psum(sum((jnp.sum(g * g) for g in gradients)), 's')]
  transfers between devices with their start and end apart: 13 -> 0, of which waited for: 7 -> 0; matrix products, arithmetic and copies ran while one was open for 48% -> 0% of each run, Pallas kernels for 0% -> 0%
where the time goes in v3:
time: 463 us
  Pallas kernels  462 us (100%)
    pallas_call x3, Pallas kernels, call(): pl.pallas_call(kernel, out_shape=[jax.ShapeDtypeStruct(*o) for o in outs]...  448 us
    pallas_call x1, Pallas kernels, update(): pl.pallas_call(functools.partial(update_kernel, count), out_shape=shapes,...  13.9 us

profile of v3, /device:TPU:0, one launch (start us, length us, event | category | flops | bytes accessed | tf_op | source)
XLA Modules:
  0.0 462.9 jit_solution(11059606149041667436)
XLA Ops:
  0.6 100.6 %shard_map.178 = (f32[10,4096,512]{2,1,0:T(8,128)}, bf16[4096,896]{1,0:T(8,128)(2,1)}, bf16[4096,896]{1,0:T(8,128)(2,1)}, bf16[896,4096]{1,0:T(8,128)(2,1)}, bf1...) custom-call(bf16[4096,896]{1,0:T(8,128)(2,1)} %bitcast.3, ...), custom_call_target="tpu_custom_call" | custom-call | tf_op jit(solution)/shard_map/pallas_call | solution.py:941
  101.2 212.3 %shard_map.179 = (bf16[112,2560]{1,0:T(8,128)(2,1)}, bf16[112,2560]{1,0:T(8,128)(2,1)}, bf16[320,896]{1,0:T(8,128)(2,1)}, bf16[4096,896]{1,0:T(8,128)(2,1)}, f32...) custom-call(bf16[4096,896]{1,0:T(8,128)(2,1)} %get-tuple-element.32., ...), custom_call_target="tpu_custom_call", output_to_operand_aliasing={{7}: (7, {}), {8}: (8, {})} | custom-call | tf_op jit(solution)/shard_map/pallas_call | solution.py:941
  313.6 135.2 %shard_map.180 = (bf16[112,2560]{1,0:T(8,128)(2,1)}, bf16[112,2560]{1,0:T(8,128)(2,1)}, bf16[320,896]{1,0:T(8,128)(2,1)}, f32[8,128]{1,0:T(8,128)}, bf16[112,256...) custom-call(bf16[896,4096]{1,0:T(8,128)(2,1)} %get-tuple-element.31., ...), custom_call_target="tpu_custom_call", output_to_operand_aliasing={{4}: (7, {}), {5}: (8, {}), {6}: (9, {})} | custom-call | tf_op jit(solution)/shard_map/pallas_call | solution.py:941
  448.8 13.9 %shard_map.181 = (bf16[2,112,2560]{2,1,0:T(8,128)(2,1)}, bf16[2,112,2560]{2,1,0:T(8,128)(2,1)}, bf16[2,320,896]{2,1,0:T(8,128)(2,1)}, f32[2,112,2560]{2,1,0:T(8,...) custom-call(f32[8,128]{1,0:T(8,128)} %get-tuple-element.46.sq_hbm, ...), custom_call_target="tpu_custom_call" | custom-call | tf_op jit(solution)/shard_map/pallas_call | solution.py:1045

commit v4 on v3

--- a/solution.py
+++ b/solution.py
@@ -368,6 +368,21 @@
                 self.home(kind, q, m).wait()
 
         self.each(m, act)
+
+    def run(self, plan):
+        for name, m in re.findall("([sfxc])([0-9]+)", plan):
+            {"s": self.spread, "f": self.forward, "x": self.cross, "c": self.complete}[name](int(m))
+
+    def follow(self, plans, t, few=5):
+        plans = plans.split("/")
+
+        def one_of(first):
+            for k, plan in enumerate(plans[first : first + few]):
+                if plan:
+                    branch(t == first + k)(lambda: self.run(plan))
+
+        for first in range(0, len(plans), few):
+            branch(both(t >= first, t < first + few))(lambda: one_of(first))
 
     def finish(self):
         for m in range(len(self.steps) - 2, len(self.steps)):
@@ -506,22 +521,7 @@
         + ((DownSteps(wd_hbm, 1, next_down_hbm, place.s, 2, down_stage), 0), (WideSteps(pair, 1, next_wide_hbm, place.s, 2, wide_stage), 0)),
         refs,
     )
-    spread, forward, cross, complete = gatherer.spread, gatherer.forward, gatherer.cross, gatherer.complete
-
-    def gather(plan):
-        for name, m in re.findall("([sfxc])([0-9]+)", plan):
-            {"s": spread, "f": forward, "x": cross, "c": complete}[name](int(m))
-
-    def follow(plans, t, few=5):
-        plans = plans.split("/")
-
-        def one_of(first):
-            for k, plan in enumerate(plans[first : first + few]):
-                if plan:
-                    branch(t == first + k)(lambda: gather(plan))
-
-        for first in range(0, len(plans), few):
-            branch(both(t >= first, t < first + few))(lambda: one_of(first))
+    gather, follow = gatherer.run, gatherer.follow
 
     def load(t):
         rows = block(t, ROWS)
@@ -660,11 +660,7 @@
         b = odd(i)
         return [local(wide_hbm.at[i], wgu.at[b], wsem.at[b, 2])] + rows_in(down_hbm, wd.at[b], wsem.at[b], i)
 
-    start(*states(0))
-    start(*weights(0))
-    for t in range(1, NT):
-        start(*states(t))
-    turned.start()
+    start(*states(0), *weights(0))
     place = Place()
     gradients = Gradients(place, refs[Gatherer.COUNT :], (gg_hbm, gu_hbm, gd_hbm), NC - 1, NC // 2 - 1)
     wides = WideSteps((wg_hbm, wu_hbm), 1, wide_hbm, place.s, 2, wide_stage, 2)
@@ -679,24 +675,8 @@
 
     loop(n_blocks, clear)
 
-    def gather_start():
-        gatherer.forward(0)
-        gatherer.spread(1)
-
-    def gather_first(i):
-        branch(i >= 1)(lambda: gatherer.cross(i))
-        branch(i >= 1)(lambda: gatherer.spread(i + 1))
-
-    def gather_last(i):
-        branch(i == 0)(lambda: gatherer.cross(0))
-        branch(i >= 1)(lambda: gatherer.forward(i + 1))
-        branch(i >= 1)(lambda: gatherer.complete(i))
-
-    def gather_between(i):
-        branch(i == 0)(lambda: gatherer.complete(0))
-        branch(i == 0)(lambda: gatherer.forward(1))
-
     def in_tiles(i):
+        gatherer.follow("f0s1/x1s2", i)
         branch(i >= 1)(lambda: gradients.wide1(i - 1))
         branch(i >= 3)(lambda: gradients.wide4(i - 3))
 
@@ -712,14 +692,17 @@
             when(i == NC - 1)(down_over.start)
 
         branch(odd(i) == 1)(odd_one)
+        branch(i == NC - 1)(lambda: gradients.wide2(i - 1))
         branch(both(odd(i) == 0, i >= 2))(lambda: gradients.down2(j - 1))
         branch(i >= 2)(lambda: gradients.wide3(i - 2))
 
     def after_wide(i):
         j = i // 2
         branch(i < NC - 1)(lambda: gradients.wide_send(i))
+        branch(i == 0)(lambda: gatherer.run("c0f1"))
         when(i == NC - 1)(wide_over.start)
-        branch(i >= 1)(lambda: gradients.wide2(i - 1))
+        branch(both(i >= 1, i < NC - 1))(lambda: gradients.wide2(i - 1))
+        branch(i == NC - 1)(lambda: gradients.wide3(i - 1))
         branch(both(odd(i) == 1, i < NC - 1))(lambda: gradients.down1(j))
         branch(both(odd(i) == 0, i >= 2))(lambda: gradients.down3(j - 1))
 
@@ -728,11 +711,15 @@
         wait(*weights(i))
 
         def tile(t):
-            when(i == 0)(lambda: wait(*states(t)))
-            branch(t == 0)(lambda: gather_first(i))
-            branch(both(t == 1, i == 0))(lambda: gather_start())
+            def load_states():
+                wait(*states(t))
+                when(t + 1 < NT)(lambda: start(*states(t + 1)))
+                when(t + 1 == NT)(turned.start)
+
+            branch(i == 0)(load_states)
+            branch(t == 0)(lambda: gatherer.follow("//x2s3/x3s4/x4s5/x5", i))
             branch(t == 2)(lambda: in_tiles(i))
-            branch(t == 3)(lambda: gather_last(i))
+            branch(t == 3)(lambda: gatherer.follow("/c1/f3c2/f4c3/f5c4/c5", i))
 
             def dots(k):
                 rows = block(2 * t + k, SUB)
@@ -754,7 +741,7 @@
         loop(NT, tile)
         gradients.put_down(i, i // 2, dot_tn(act_ref[...], dy_ref[...]))
         after_down(i)
-        gather_between(i)
+        gatherer.follow("x0/f2", i)
         when(i + 1 < NC)(lambda: start(*weights(i + 1)))
         when(i == 0)(turned.wait)
         gradients.put_wide(i, dot(aT_ref[...], dgu_ref[...]))
@@ -774,14 +761,12 @@
         da = wide(da_ref[rows, :].astype(bf16))
         scale = norm_scale(w)
         along = jnp.sum(da * w, -1, keepdims=True) * (scale * scale * scale) * (1.0 / D)
-        by_h = (da * scale - w * along).astype(bf16)
-        dy_ref[rows, :] = (wide(dy_ref[rows, :]) + wide(by_h)).astype(bf16)
+        dy_ref[rows, :] = (wide(dy_ref[rows, :]) + (da * scale - w * along)).astype(bf16)
         store(t).start()
-        branch(t == n_blocks // 2)(lambda: gradients.wide3(NC - 2))
+        branch(t == n_blocks // 2)(lambda: gradients.wide4(NC - 2))
 
     gradients.wide4(NC - 3)
     loop(n_blocks, norm_back)
-    gradients.wide4(NC - 2)
     sq[...] = gradients.squares()
     done = local(sq, sq_hbm, qsem)
     done.start()
@@ -814,11 +799,7 @@
     def kept(n):
         return local(kept_hbm.at[n // NT, block(n % NT, TM), :], gus.at[n % depth], gsem.at[n % depth])
 
-    start(*weights(0))
-    for t in range(NT):
-        start(states(t), turned(t))
-        if t < depth:
-            kept(t).start()
+    start(*weights(0), states(0), kept(0))
     before = local(sq_in, sq, qsem)
     before.start()
     place = Place()
@@ -847,15 +828,22 @@
         some = before is not None
         i, t = n // NT, n % NT
         q = i // 2
-        when(n < NT)(lambda: states(t).wait())
-        if some:
-            when(n <= NT)(lambda: turned(n - 1).wait())
+
+        def load_states():
+            when(n < NT)(lambda: states(t).wait())
+            if some:
+                turned(n - 1).wait()
+            when(n + 1 < NT)(lambda: start(states(n + 1)))
+            when(n < NT)(lambda: start(turned(n)))
+            when(n + 1 < depth)(lambda: kept(n + 1).start())
+
+        branch(n <= NT)(load_states)
 
         def next_weights():
             wait(*weights(i))
             when(i + 1 < NC)(lambda: start(*weights(i + 1)))
 
-        when(t == 0)(next_weights)
+        branch(t == 0)(next_weights)
         kept(n).wait()
         last = (t + NT - 1) % NT
         fresh = last == 0 if before is evens else None
@@ -904,28 +892,31 @@
         step(2 * p + 1, odds, evens)
         step(2 * p + 2, evens, odds)
 
+    step(0, evens, None)
     wait(*left)
     gradients.wide_send(0)
     gradients.down_send(0)
-    step(0, evens, None)
     loop(NC * NT // 2 - 1, two_steps)
     step(NC * NT - 1 + place.s * 0, odds, evens)
     end, q = NC, NC // 2
     terms_d(NT - 1, odd_act)
+    gradients.down4(q - 1)
+    gradients.put_down(NC - 1, q, by_d[...])
+    gradients.down_send(q)
     terms_gu(NT - 1, odd_dgu)
-    gradients.down4(q - 1)
-    ended(NC - 1)
+    gradients.put_wide(end, by_gu[...])
+    gradients.wide_send(end)
+    gradients.down1(q)
     gradients.wide3(end - 1)
-    before.wait()
     gradients.wide1(end)
-    gradients.down1(q)
+    gradients.down2(q)
     gradients.wide4(end - 1)
     gradients.wide2(end)
-    gradients.down2(q)
+    gradients.down3(q)
     gradients.wide3(end)
-    gradients.down3(q)
+    before.wait()
+    gradients.down4(q)
     gradients.wide4(end)
-    gradients.down4(q)
     sq[...] += gradients.squares()
     exchanges = [remote(sq, parts.at[n], psem.at[0, n], psem.at[1, n], {"s": s}) for n, s in enumerate(place.peers)]
     start(*exchanges)

time: 463 us -> 452 us (0.976)
  Pallas kernels: 462 us -> 451 us
    pallas_call x3, Pallas kernels: 448 us -> 437 us  [call(): pl.pallas_call(kernel, out_shape=[jax.ShapeDtypeStruct(*o) for o in outs]...]
where the time goes in v4:
time: 452 us
  Pallas kernels  451 us (100%)
    pallas_call x3, Pallas kernels, call(): pl.pallas_call(kernel, out_shape=[jax.ShapeDtypeStruct(*o) for o in outs]...  437 us
    pallas_call x1, Pallas kernels, update(): pl.pallas_call(functools.partial(update_kernel, count), out_shape=shapes,...  13.9 us

profile of v4, /device:TPU:0, one launch (start us, length us, event | category | flops | bytes accessed | tf_op | source)
XLA Modules:
  0.0 451.9 jit_solution(4238445805194631307)
XLA Ops:
  0.6 100.6 %shard_map.178 = (f32[10,4096,512]{2,1,0:T(8,128)}, bf16[4096,896]{1,0:T(8,128)(2,1)}, bf16[4096,896]{1,0:T(8,128)(2,1)}, bf16[896,4096]{1,0:T(8,128)(2,1)}, bf1...) custom-call(bf16[4096,896]{1,0:T(8,128)(2,1)} %bitcast.3, ...), custom_call_target="tpu_custom_call" | custom-call | tf_op jit(solution)/shard_map/pallas_call | solution.py:932
  101.2 206.4 %shard_map.179 = (bf16[112,2560]{1,0:T(8,128)(2,1)}, bf16[112,2560]{1,0:T(8,128)(2,1)}, bf16[320,896]{1,0:T(8,128)(2,1)}, bf16[4096,896]{1,0:T(8,128)(2,1)}, f32...) custom-call(bf16[4096,896]{1,0:T(8,128)(2,1)} %get-tuple-element.32., ...), custom_call_target="tpu_custom_call", output_to_operand_aliasing={{7}: (7, {}), {8}: (8, {})} | custom-call | tf_op jit(solution)/shard_map/pallas_call | solution.py:932
  307.6 130.2 %shard_map.180 = (bf16[112,2560]{1,0:T(8,128)(2,1)}, bf16[112,2560]{1,0:T(8,128)(2,1)}, bf16[320,896]{1,0:T(8,128)(2,1)}, f32[8,128]{1,0:T(8,128)}, bf16[112,256...) custom-call(bf16[896,4096]{1,0:T(8,128)(2,1)} %get-tuple-element.31., ...), custom_call_target="tpu_custom_call", output_to_operand_aliasing={{4}: (7, {}), {5}: (8, {}), {6}: (9, {})} | custom-call | tf_op jit(solution)/shard_map/pallas_call | solution.py:932
  437.8 13.9 %shard_map.181 = (bf16[2,112,2560]{2,1,0:T(8,128)(2,1)}, bf16[2,112,2560]{2,1,0:T(8,128)(2,1)}, bf16[2,320,896]{2,1,0:T(8,128)(2,1)}, f32[2,112,2560]{2,1,0:T(8,...) custom-call(f32[8,128]{1,0:T(8,128)} %get-tuple-element.46.sq_hbm, ...), custom_call_target="tpu_custom_call" | custom-call | tf_op jit(solution)/shard_map/pallas_call | solution.py:1036
